TPU v7x, 32 devices: a whole 2x2x4 slice. The times are simulated.
32 devices in a mesh: blocks: 8 (over z, x), gz: 4 (over y, core).
Axes of the slice: x: 2, y: 2, z: 4, core: 2. Of those that a mesh axis runs over, the one named last changes fastest.
Arguments:
- coarse_field: float32 [4, 128, 3, 4096], P('gz', 'blocks'), may hold values from -6 to 6
- coarse_velocity: float32 [4, 128, 3, 4096], P('gz', 'blocks'), may hold values from -15 to 15
- fine_field: float32 [4, 96, 3, 4096], P('gz', 'blocks'), may hold values from -6 to 6
- fine_velocity: float32 [4, 96, 3, 4096], P('gz', 'blocks'), may hold values from -15 to 15
- pairs: int32 [4, 32, 6], P('gz', 'blocks'), may hold values from 0 to 15, as said below
Outputs:
- coarse_new: float32 [4, 128, 3, 4096], P('gz', 'blocks')
- fine_new: float32 [4, 96, 3, 4096], P('gz', 'blocks')
- face_jump: float32 [4, 32, 256], P('gz', 'blocks')
Inputs may be any that keep to these rules, and one draw needn't show every extreme that they name: `pairs`: Columns: fine slot below 12, face axis 0 to 2, owner device below 8, coarse slot below 16, quadrant row and column 0 or 1. No two rows of a device name the same fine slot and face axis, and no two rows of a group name the same coarse block, face axis and quadrant. The rows of one device name one owner device at most 2 times, and exactly 2 times for some owner; rows of one device that name the same owner differ in face axis; some owner is named 2 times by every device of its group. Each face axis stands in 1 to 2 of a device's rows.
All inputs are finite; a program needn't handle non-finite values.
Results may differ from a plain program's by a relative error of at most 0.0003.
Values sent between devices are 32-bit elements; how exact they have to be, the bound alone decides.
A program may use at most 256 MiB of HBM per device.

v0:
```python
import functools

import jax
import jax.numpy as jnp
from jax import lax
from jax.experimental import pallas as pl
from jax.experimental.pallas import tpu as pltpu
from jax.sharding import PartitionSpec as P

EDGE = 16
HALF = 8
CAP = 2
LANES = 128
ROWS = 8
TILES = EDGE**3 // LANES
BIG = 1e30
EMPTY = 3e38
TANGENT = ((1, 2), (0, 2), (0, 1))
MESH = pl.DeviceIdType.MESH


def take(values, index):
    return jnp.take_along_axis(values, index, axis=1, mode="promise_in_bounds")


def kernel(
    peers,
    groups,
    coarse_count,
    fine_count,
    pair_count,
    pairs_hbm,
    cb_hbm,
    cv_hbm,
    fb_hbm,
    fv_hbm,
    curl_c,
    curl_f,
    jump_out,
    pairs,
    cb,
    cv,
    fb,
    fv,
    emf_c,
    emf_f,
    tab_r,
    tab_n,
    rep,
    own,
    picked,
    send1,
    recv1,
    send2,
    recv2,
    gmax,
    gmax_in,
    load_sem,
    s1_sem,
    r1_sem,
    s2_sem,
    r2_sem,
    sg_sem,
    rg_sem,
):
    me = lax.axis_index("blocks")
    mg = lax.axis_index("gz")
    few = peers <= 8

    def each_peer(body):
        lax.fori_loop(1, peers, lambda k, _: (body(lax.rem(me + k, peers)), 0)[1], 0, unroll=few)

    def each_group(body):
        for k in range(1, groups):
            body(lax.rem(mg + k, groups))

    loads = [
        pltpu.make_async_copy(src, dst, load_sem.at[n])
        for n, (src, dst) in enumerate(((fb_hbm, fb), (fv_hbm, fv), (cb_hbm, cb), (cv_hbm, cv)))
    ]
    listed = pltpu.make_async_copy(pairs_hbm, pairs, load_sem.at[4])
    listed.start()
    for load in loads:
        load.start()
    barrier = pltpu.get_barrier_semaphore()
    each_peer(
        lambda p: pl.semaphore_signal(barrier, inc=1, device_id=(p, mg), device_id_type=MESH)
    )
    each_group(
        lambda g: pl.semaphore_signal(barrier, inc=1, device_id=(me, g), device_id_type=MESH)
    )

    lane = lax.broadcasted_iota(jnp.int32, (ROWS, LANES), 1)
    sub = lax.broadcasted_iota(jnp.int32, (ROWS, LANES), 0)
    k_of = lane % EDGE
    first_y = lane < EDGE
    last_y = lane >= LANES - EDGE
    first_z = k_of == 0
    last_z = k_of == EDGE - 1

    def back_y(pair):
        low, high = pltpu.roll(pair[0], EDGE, 1), pltpu.roll(pair[1], EDGE, 1)
        return jnp.where(first_y, high, low), jnp.where(first_y, low, high)

    def ahead_y(pair):
        low, high = pltpu.roll(pair[0], LANES - EDGE, 1), pltpu.roll(pair[1], LANES - EDGE, 1)
        return jnp.where(last_y, high, low), jnp.where(last_y, low, high)

    def back_z(pair):
        return tuple(
            jnp.where(first_z, pltpu.roll(v, LANES - EDGE + 1, 1), pltpu.roll(v, 1, 1))
            for v in pair
        )

    def ahead_z(pair):
        return tuple(
            jnp.where(last_z, pltpu.roll(v, EDGE - 1, 1), pltpu.roll(v, LANES - 1, 1))
            for v in pair
        )

    def add(a, b):
        return a[0] + b[0], a[1] + b[1]

    def sub2(a, b):
        return a[0] - b[0], a[1] - b[1]

    def mul(a, b):
        return a[0] * b[0], a[1] * b[1]

    def scale(s, a):
        return s * a[0], s * a[1]

    def column(tile):
        return pl.ds(pl.multiple_of(tile * LANES, LANES), LANES)

    def blocked(ref, g):
        def read(c, i):
            return tuple(ref[c, ROWS * g : ROWS * g + ROWS, column(2 * i + h)] for h in range(2))

        return read

    def strided(ref, start):
        def read(c, i):
            return tuple(
                ref[pl.ds(start * 3 * TILES + c * TILES + 2 * i + h, ROWS, stride=3 * TILES), :]
                for h in range(2)
            )

        return read

    def blocked_put(ref, g):
        def put(c, i, pair):
            for h in range(2):
                ref[c, ROWS * g : ROWS * g + ROWS, column(2 * i + h)] = pair[h]

        return put

    def strided_put(ref, start):
        def put(c, i, pair):
            for h in range(2):
                ref[pl.ds(start * 3 * TILES + c * TILES + 2 * i + h, ROWS, stride=3 * TILES), :] = (
                    pair[h]
                )

        return put

    def cells(field, velocity, i, want_speed):
        after = lax.rem(i + 1, EDGE)
        b_x, b_y, b_z = field(0, i), field(1, i), field(2, i)
        c_x = scale(0.5, add(b_x, field(0, after)))
        c_y = scale(0.5, add(b_y, ahead_y(b_y)))
        c_z = scale(0.5, add(b_z, ahead_z(b_z)))
        v_x, v_y, v_z = velocity(0, i), velocity(1, i), velocity(2, i)
        cell_y = sub2(mul(v_x, c_z), mul(v_z, c_x))
        cell_z = sub2(mul(v_y, c_x), mul(v_x, c_y))
        part_y = scale(0.25, add(cell_y, back_z(cell_y)))
        part_z = scale(0.25, add(cell_z, back_y(cell_z)))
        if not want_speed:
            return part_y, part_z
        cell_x = sub2(mul(v_z, c_y), mul(v_y, c_z))
        part_x = scale(0.25, add(cell_x, back_y(cell_x)))
        e_x = add(part_x, back_z(part_x))
        vv = add(add(mul(v_x, v_x), mul(v_y, v_y)), mul(v_z, v_z))
        cc = add(add(mul(c_x, c_x), mul(c_y, c_y)), mul(c_z, c_z))
        speed = jnp.maximum(
            jnp.sqrt(vv[0]) + jnp.sqrt(cc[0]), jnp.sqrt(vv[1]) + jnp.sqrt(cc[1])
        )
        return part_y, part_z, e_x, speed

    def emf_pass(sources, target, best):
        starts = [cells(f, v, EDGE - 1, False) for f, v in sources]

        def step(i, carry):
            parts, top = carry
            fresh = []
            for g, (f, v) in enumerate(sources):
                part_y, part_z, e_x, speed = cells(f, v, i, True)
                put = blocked_put(target, g)
                put(0, i, e_x)
                put(1, i, add(part_y, parts[g][0]))
                put(2, i, add(part_z, parts[g][1]))
                top = jnp.maximum(top, speed)
                fresh.append((part_y, part_z))
            return fresh, top

        return lax.fori_loop(0, EDGE, step, (starts, best))[1]

    def curl_pass(emf, puts):
        def step(i, carry):
            after = lax.rem(i + 1, EDGE)
            for g, put in enumerate(puts):
                read = blocked(emf, g)
                e_x, e_y, e_z = read(0, i), read(1, i), read(2, i)
                put(0, i, sub2(sub2(ahead_y(e_z), e_z), sub2(ahead_z(e_y), e_y)))
                put(1, i, sub2(sub2(ahead_z(e_x), e_x), sub2(read(2, after), e_z)))
                put(2, i, sub2(sub2(read(1, after), e_y), sub2(ahead_y(e_x), e_x)))
            return carry

        lax.fori_loop(0, EDGE, step, 0)

    coarse_groups = coarse_count // ROWS
    fine_groups = -(-fine_count // ROWS)
    fine_starts = [min(ROWS * g, fine_count - ROWS) for g in range(fine_groups)]
    fine_rows = ROWS * fine_groups

    def fine_row(slot):
        last = ROWS * (fine_groups - 1)
        return jnp.where(slot < last, slot, slot - fine_starts[-1] + last)

    loads[0].wait()
    loads[1].wait()
    best = emf_pass([(strided(fb, s), strided(fv, s)) for s in fine_starts], emf_f, jnp.zeros((ROWS, LANES), jnp.float32))

    within = lane % 64
    row_m, col_n = within // HALF, within % HALF
    face_x = (row_m % 4) * 32 + col_n * 2
    for g in range(fine_groups):
        read = blocked(emf_f, g)
        for d in range(3):
            kept = []
            for which in range(2):
                axis = TANGENT[d][which]
                acc = jnp.zeros((ROWS, LANES), jnp.float32)
                if d == 0:
                    pair = read(axis, 0)
                    shift = EDGE if which == 0 else 1
                    for h in range(2):
                        mean = 0.5 * (pair[h] + pltpu.roll(pair[h], LANES - shift, 1))
                        acc = jnp.where(row_m // 4 == h, take(mean, face_x), acc)
                elif d == 1:
                    for m in range(HALF):
                        here = read(axis, 2 * m)[0]
                        other = read(axis, 2 * m + 1)[0] if which == 0 else pltpu.roll(here, LANES - 1, 1)
                        acc = jnp.where(row_m == m, take(0.5 * (here + other), col_n * 2), acc)
                else:
                    for m in range(HALF):
                        here = read(axis, 2 * m)
                        other = read(axis, 2 * m + 1) if which == 0 else [pltpu.roll(v, LANES - EDGE, 1) for v in here]
                        for h in range(2):
                            got = take(0.5 * (here[h] + other[h]), (col_n % 4) * 32)
                            acc = jnp.where((row_m == m) & (col_n // 4 == h), got, acc)
                kept.append(acc)
            tab_r[d * fine_rows + ROWS * g : d * fine_rows + ROWS * g + ROWS, :] = jnp.where(
                lane < 64, kept[0], kept[1]
            )

    listed.wait()
    slot_of = [pairs[r, 0] for r in range(pair_count)]
    face_of = [pairs[r, 1] for r in range(pair_count)]
    owner_of = [pairs[r, 2] for r in range(pair_count)]
    table_row = [face_of[r] * fine_rows + fine_row(slot_of[r]) for r in range(pair_count)]
    message_row = []
    for r in range(pair_count):
        rank = jnp.int32(0)
        for q in range(r):
            rank = rank + jnp.where(owner_of[q] == owner_of[r], 1, 0)
        message_row.append(owner_of[r] * ROWS + rank)

    box = lax.broadcasted_iota(jnp.int32, (peers * ROWS, LANES), 0)
    message = jnp.full((peers * ROWS, LANES), -1.0, jnp.float32)
    for r in range(pair_count):
        code = pairs[r, 3] * 12 + face_of[r] * 4 + pairs[r, 4] * 2 + pairs[r, 5]
        values = tab_r[pl.ds(table_row[r], 1), :]
        message = jnp.where(box == message_row[r], values, message)
        message = jnp.where(box == message_row[r] + CAP, code.astype(jnp.float32), message)
    send1[...] = message

    pl.semaphore_wait(barrier, peers - 1 + groups - 1)

    def slot(ref, p):
        return ref.at[pl.ds(pl.multiple_of(p * ROWS, ROWS), ROWS)]

    def out1(p):
        return pltpu.make_async_remote_copy(
            src_ref=slot(send1, p), dst_ref=slot(recv1, me), send_sem=s1_sem,
            recv_sem=r1_sem, device_id=(p, mg), device_id_type=MESH,
        )

    def out2(p):
        return pltpu.make_async_remote_copy(
            src_ref=slot(send2, p), dst_ref=slot(recv2, me), send_sem=s2_sem,
            recv_sem=r2_sem, device_id=(p, mg), device_id_type=MESH,
        )

    def outg(g):
        return pltpu.make_async_remote_copy(
            src_ref=gmax, dst_ref=slot(gmax_in, mg), send_sem=sg_sem,
            recv_sem=rg_sem, device_id=(me, g), device_id_type=MESH,
        )

    def drain(ref, sem, count):
        part = ref.at[pl.ds(0, ROWS * count)]
        pltpu.make_async_copy(part, part, sem).wait()

    each_peer(lambda p: out1(p).start())

    loads[2].wait()
    loads[3].wait()
    best = emf_pass([(blocked(cb, g), blocked(cv, g)) for g in range(coarse_groups)], emf_c, best)
    gmax[...] = best
    each_group(lambda g: outg(g).start())

    curl_pass(emf_f, [strided_put(curl_f, s) for s in fine_starts])


    def gathered_rows(read, d, h):
        out = jnp.zeros((ROWS, LANES), jnp.float32)
        for m in range(HALF):
            here = read(d, h * HALF + m)[0]
            out = jnp.where(lane // EDGE == m, here if m == 0 else pltpu.roll(here, EDGE * m, 1), out)
        return out

    def normal_curl(g):
        edge = blocked(emf_c, g)

        def read(d, i):
            after = (i + 1) % EDGE
            if d == 0:
                e_y, e_z = edge(1, i), edge(2, i)
                return sub2(sub2(ahead_y(e_z), e_z), sub2(ahead_z(e_y), e_y))
            if d == 1:
                e_x, e_z = edge(0, i)[:1], edge(2, i)
                return ((ahead_z(e_x)[0] - e_x[0]) - (edge(2, after)[0] - e_z[0]),)
            e_x, e_y = edge(0, i), edge(1, i)
            return sub2(sub2(edge(1, after), e_y), sub2(ahead_y(e_x), e_x))

        return read

    def quadrants(read, g, second):
        def put(d, q1, q2, value):
            n = (g * 12 + d * 4 + q1 * 2 + q2) * ROWS
            if second:
                value = jnp.where(lane < 64, rep[n : n + ROWS, :], value)
            rep[n : n + ROWS, :] = value

        plane = read(0, 0)
        for d in range(2):
            for q1 in range(2):
                face = plane[q1] if d == 0 else gathered_rows(read, 1, q1)
                for q2 in range(2):
                    put(d, q1, q2, take(face, row_m * EDGE + q2 * HALF + col_n))
        for q1 in range(2):
            got = [jnp.zeros((ROWS, LANES), jnp.float32)] * 2
            for m in range(HALF):
                pair = read(2, q1 * HALF + m)
                got = [
                    jnp.where(row_m == m, take(pair[q2], col_n * EDGE), got[q2]) for q2 in range(2)
                ]
            for q2 in range(2):
                put(2, q1, q2, got[q2])

    for g in range(coarse_groups):
        quadrants(blocked(cb, g), g, False)

    slot(recv1, me)[...] = slot(send1, me)[...]
    drain(recv1, r1_sem, peers - 1)
    codes = [
        [((sub + ROWS * g) * 12 + dq).astype(jnp.float32) for dq in range(12)]
        for g in range(coarse_groups)
    ]

    def row_of(ref, n):
        return jnp.broadcast_to(ref[pl.ds(n, 1), :], (ROWS, LANES))

    def collect(p, held):
        for c in range(CAP):
            values, key = row_of(recv1, p * ROWS + c), row_of(recv1, p * ROWS + CAP + c)
            held = [
                [jnp.where(key == codes[g][dq], values, held[g][dq]) for dq in range(12)]
                for g in range(coarse_groups)
            ]
        return held

    empty = jnp.full((ROWS, LANES), EMPTY, jnp.float32)
    held = lax.fori_loop(0, peers, collect, [[empty] * 12 for _ in range(coarse_groups)], unroll=few)
    halves = k_of < HALF
    for g in range(coarse_groups):
        def patch(axis, tile, value, mask):
            where = (axis, slice(ROWS * g, ROWS * g + ROWS), slice(tile * LANES, tile * LANES + LANES))
            put = value < BIG
            if mask is not None:
                put = put & mask
            emf_c[where] = jnp.where(put, value, emf_c[where])

        for d in range(3):
            for which in range(2):
                axis = TANGENT[d][which]
                for q1 in range(2):
                    low, high = held[g][d * 4 + q1 * 2], held[g][d * 4 + q1 * 2 + 1]
                    if d < 2:
                        spread = (lane // EDGE) * HALF + lane % HALF + 64 * which
                        both = jnp.where(halves, take(low, spread), take(high, spread))
                        if d == 0:
                            patch(axis, q1, both, None)
                        else:
                            for m in range(HALF):
                                turned = both if m == 0 else pltpu.roll(both, LANES - EDGE * m, 1)
                                patch(axis, 2 * (q1 * HALF + m), turned, first_y)
                    else:
                        for m in range(HALF):
                            for q2 in range(2):
                                got = take((low, high)[q2], m * HALF + lane // EDGE + 64 * which)
                                patch(axis, 2 * (q1 * HALF + m) + q2, got, first_z)

    for g in range(coarse_groups):
        quadrants(normal_curl(g), g, True)

    drain(gmax_in, rg_sem, groups - 1)
    for k in range(1, groups):
        best = jnp.maximum(best, slot(gmax_in, lax.rem(mg + k, groups))[...])
    top_row = jnp.max(best, axis=0, keepdims=True)

    def answer(p, carry):
        rows = jnp.broadcast_to(top_row, (ROWS, LANES))
        for c in range(CAP):
            key = row_of(recv1, p * ROWS + CAP + c)
            acc = jnp.zeros((ROWS, LANES), jnp.float32)
            for g in range(coarse_groups):
                for dq in range(12):
                    acc = jnp.where(
                        key == codes[g][dq],
                        rep[(g * 12 + dq) * ROWS : (g * 12 + dq + 1) * ROWS, :],
                        acc,
                    )
            rows = jnp.where(sub == c, jnp.sum(acc, axis=0, keepdims=True), rows)
        slot(send2, p)[...] = rows
        return carry

    lax.fori_loop(0, peers, answer, 0, unroll=few)
    each_peer(lambda p: out2(p).start())
    curl_pass(emf_c, [blocked_put(curl_c, g) for g in range(coarse_groups)])

    for g in range(fine_groups):
        for n, read in enumerate((strided(fb, fine_starts[g]), strided(curl_f, fine_starts[g]))):
            for d in range(3):
                for h in range(2):
                    if d == 0:
                        face = read(0, 0)[h]
                    elif d == 1:
                        face = gathered_rows(read, 1, h)
                    else:
                        face = jnp.zeros((ROWS, LANES), jnp.float32)
                        for m in range(HALF):
                            pair = read(2, h * HALF + m)
                            for part in range(2):
                                face = jnp.where(
                                    (lane // EDGE == m) & (k_of // HALF == part),
                                    take(pair[part], (lane % HALF) * EDGE),
                                    face,
                                )
                    tab_n[
                        d * fine_rows + ROWS * g : d * fine_rows + ROWS * g + ROWS,
                        (2 * n + h) * LANES : (2 * n + h + 1) * LANES,
                    ] = face
    for r in range(pair_count):
        picked[r : r + 1, :] = tab_n[pl.ds(table_row[r], 1), :]

    slot(recv2, me)[...] = slot(send2, me)[...]
    drain(recv2, r2_sem, peers - 1)
    top = jnp.full((ROWS, LANES), 0.0, jnp.float32)
    top = lax.fori_loop(0, peers, lambda p, t: jnp.maximum(t, row_of(recv2, p * ROWS + CAP)), top, unroll=few)
    dt = 0.2 / jnp.max(top, axis=1, keepdims=True)
    for r in range(pair_count):
        own[r : r + 1, :] = recv2[pl.ds(message_row[r], 1), :]
    for s in range(0, pair_count, ROWS):
        take_rows = min(ROWS, pair_count - s)
        quad = own[s : s + ROWS, :]
        quad = quad - dt * pltpu.roll(quad, 64, 1)
        for h in range(2):
            coarse = take(quad, (4 * h + lane // 32) * HALF + k_of // 2)
            fine = picked[s : s + ROWS, h * LANES : (h + 1) * LANES] - (dt / 0.5) * picked[
                s : s + ROWS, (2 + h) * LANES : (3 + h) * LANES
            ]
            jump_out[s : s + take_rows, h * LANES : (h + 1) * LANES] = (fine - coarse)[:take_rows]

    def finish(i, carry):
        for g in range(coarse_groups):
            read, put, curl = blocked(cb, g), blocked_put(curl_c, g), blocked(curl_c, g)
            for c in range(3):
                put(c, i, sub2(read(c, i), (dt * curl(c, i)[0], dt * curl(c, i)[1])))
        return carry

    lax.fori_loop(0, EDGE, finish, 0, unroll=2)
    doubled = dt / 0.5
    span = fine_count * 3 * ROWS

    def finish_fine(n, carry):
        part = pl.ds(pl.multiple_of(n * span, ROWS), span)
        curl_f[part, :] = fb[part, :] - doubled[:1] * curl_f[part, :]
        return carry

    lax.fori_loop(0, TILES // ROWS, finish_fine, 0)
    drain(send1, s1_sem, peers - 1)
    drain(send2, s2_sem, peers - 1)
    drain(gmax_in, sg_sem, groups - 1)


def store(curl_c, curl_f, jump, out_c, out_f, out_j, sems):
    copies = [
        pltpu.make_async_copy(src, dst, sems.at[n])
        for n, (src, dst) in enumerate(((curl_c, out_c), (curl_f, out_f), (jump, out_j)))
    ]
    for copy in copies:
        copy.start()
    for copy in copies:
        copy.wait()


def on_device(peers, groups, coarse_field, coarse_velocity, fine_field, fine_velocity, pairs):
    coarse_count, fine_count = coarse_field.shape[1], fine_field.shape[1]
    pair_count = pairs.shape[1]
    cells = EDGE**3
    flat_rows = fine_count * 3 * TILES

    def coarse_view(x):
        return jnp.transpose(x[0], (1, 0, 2))

    def fine_view(x):
        return x.reshape(flat_rows, LANES)

    fine_rows = ROWS * -(-fine_count // ROWS)
    pair_rows = ROWS * -(-pair_count // ROWS)
    cb, cv = coarse_view(coarse_field), coarse_view(coarse_velocity)
    fb, fv = fine_view(fine_field), fine_view(fine_velocity)
    operands = [
        pltpu.with_memory_space_constraint(x, pltpu.HBM) for x in (pairs[0], cb, cv, fb, fv)
    ]
    f32 = jnp.float32
    dma = pltpu.SemaphoreType.DMA
    vmem = pltpu.VMEM
    anywhere = pl.BlockSpec(memory_space=pltpu.HBM)
    inside = pl.BlockSpec(memory_space=pltpu.VMEM)
    coarse_shape, fine_shape = (3, coarse_count, cells), (flat_rows, LANES)
    new_c, new_f, jump = pl.pallas_call(
        functools.partial(kernel, peers, groups, coarse_count, fine_count, pair_count),
        out_shape=(
            jax.ShapeDtypeStruct(coarse_shape, f32),
            jax.ShapeDtypeStruct(fine_shape, f32),
            jax.ShapeDtypeStruct((pair_count, EDGE * EDGE), f32),
        ),
        in_specs=[anywhere] * 5,
        out_specs=(inside,) * 3,
        scratch_shapes=[
            pltpu.SMEM(pairs.shape[1:], jnp.int32),
            vmem(coarse_shape, f32),
            vmem(coarse_shape, f32),
            vmem(fine_shape, f32),
            vmem(fine_shape, f32),
            vmem(coarse_shape, f32),
            vmem((3, fine_rows, cells), f32),
            vmem((3 * fine_rows, LANES), f32),
            vmem((3 * fine_rows, 4 * LANES), f32),
            vmem((12 * coarse_count, LANES), f32),
            vmem((pair_rows, LANES), f32),
            vmem((pair_rows, 4 * LANES), f32),
            vmem((peers * ROWS, LANES), f32),
            vmem((peers * ROWS, LANES), f32),
            vmem((peers * ROWS, LANES), f32),
            vmem((peers * ROWS, LANES), f32),
            vmem((ROWS, LANES), f32),
            vmem((groups * ROWS, LANES), f32),
            dma((5,)),
            dma,
            dma,
            dma,
            dma,
            dma,
            dma,
        ],
        compiler_params=pltpu.CompilerParams(
            collective_id=0, has_side_effects=True, vmem_limit_bytes=32 * 1024 * 1024
        ),
    )(*operands)
    coarse_out, fine_out, jump = pl.pallas_call(
        store,
        out_shape=(
            jax.ShapeDtypeStruct(coarse_shape, f32),
            jax.ShapeDtypeStruct(fine_shape, f32),
            jax.ShapeDtypeStruct((pair_count, EDGE * EDGE), f32),
        ),
        in_specs=[inside] * 3,
        out_specs=(anywhere,) * 3,
        scratch_shapes=[dma((3,))],
    )(*(pltpu.with_memory_space_constraint(x, pltpu.VMEM) for x in (new_c, new_f, jump)))
    return (
        jnp.transpose(coarse_out, (1, 0, 2))[None],
        fine_out.reshape(1, fine_count, 3, cells),
        jump[None],
    )


def solution(mesh):
    spec = P("gz", "blocks", None, None)
    flat = P("gz", "blocks", None)
    return jax.shard_map(
        functools.partial(on_device, mesh.shape["blocks"], mesh.shape["gz"]),
        mesh=mesh,
        in_specs=(spec, spec, spec, spec, flat),
        out_specs=(spec, spec, flat),
        check_vma=False,
    )
```

profile of v0, /device:TPU:0, one launch (start us, length us, event | category | flops | bytes accessed | tf_op | source)
XLA Modules:
  0.0 27.2 jit_solution(3803413522563392163)
XLA Ops:
  0.6 25.5 %shard_map.76 = (f32[3,16,4096]{2,1,0:T(8,128)S(1)}, f32[1152,128]{1,0:T(8,128)S(1)}, f32[4,256]{1,0:T(4,128)S(1)}) custom-call(s32[4,6]{1,0:T(4,128)} %bitcast.18, f32[3,16,4096]{2,1,0:T(8,128)} %bitcast.14, f32[3,16,4096]{2,1,0:T(8,128)} %bitcast.15, f32[1152,128]{1,0:T(8,128)} %bitcast.16, f32[1152,128]{1,0:T(8,128)} %bitcast.17), custom_call_target="tpu_custom_call" | custom-call | tf_op jit(solution)/shard_map/pallas_call | solution.py:554
  26.1 1.1 %shard_map.77 = (f32[3,16,4096]{2,1,0:T(8,128)}, f32[1152,128]{1,0:T(8,128)}, f32[4,256]{1,0:T(4,128)}) custom-call(f32[3,16,4096]{2,1,0:T(8,128)S(1)} %get-tuple-element.9.curl_c, f32[1152,128]{1,0:T(8,128)S(1)} %get-tuple-element.10.curl_f, f32[4,256]{1,0:T(4,128)S(1)} %get-tuple-element.11.jump), custom_call_target="tpu_custom_call" | custom-call | tf_op jit(solution)/shard_map/pallas_call | solution.py:594
where the time goes:
time: 27.4 us; the launch traced here: 27.2 us
  Pallas kernels  26.6 us (97%)
  between operations  0.64 us (2%)
    pallas_call x1, Pallas kernels, on_device(): pl.pallas_call(functools.partial(kernel, peers, groups, coarse_count, fin...  25.5 us
    pallas_call x1, Pallas kernels, on_device(): pl.pallas_call(store, out_shape=(jax.ShapeDtypeStruct(coarse_shape, f32),...  1.1 us

commit v1 on v0

v1 whole, which is shorter than its diff:
```python
import functools

import jax
import jax.numpy as jnp
from jax import lax
from jax.experimental import pallas as pl
from jax.experimental.pallas import tpu as pltpu
from jax.sharding import PartitionSpec as P

EDGE = 16
HALF = 8
CAP = 2
LANES = 128
ROWS = 8
TILES = EDGE**3 // LANES
SPAN = 3 * TILES
TINY = 1.2e-38
BIG = 1e30
EMPTY = 3e38
TANGENT = ((1, 2), (0, 2), (0, 1))
MESH = pl.DeviceIdType.MESH
COARSE_STEP = 8
FINE_STEP = 4


def take(values, index):
    return jnp.take_along_axis(values, index, axis=1, mode="promise_in_bounds")


def largest_step(count, most):
    return max(n for n in range(1, most + 1) if count % n == 0)


def kernel(
    peers,
    groups,
    coarse_count,
    fine_count,
    pair_count,
    pairs_hbm,
    cb_hbm,
    cv_hbm,
    fb_hbm,
    fv_hbm,
    cb,
    curl_c,
    fb,
    curl_f,
    jump_a,
    jump_b,
    step_out,
    pairs,
    cv,
    fv,
    emf_c,
    emf_p,
    plane_e,
    plane_b,
    plane_n,
    held_ref,
    own_a,
    own_b,
    picked,
    rows1,
    send1,
    recv1,
    send2,
    recv2,
    gmax,
    gmax_in,
    load_sem,
    s1_sem,
    r1_sem,
    s2_sem,
    r2_sem,
    sg_sem,
    rg_sem,
):
    me = lax.axis_index("blocks")
    mg = lax.axis_index("gz")
    few = peers <= 8
    coarse_groups = coarse_count // ROWS
    pair_rows = ROWS * -(-pair_count // ROWS)

    def each_peer(body):
        lax.fori_loop(1, peers, lambda k, _: (body(lax.rem(me + k, peers)), 0)[1], 0, unroll=few)

    def each_group(body):
        for k in range(1, groups):
            body(lax.rem(mg + k, groups))

    barrier = pltpu.get_barrier_semaphore()
    each_peer(
        lambda p: pl.semaphore_signal(barrier, inc=1, device_id=(p, mg), device_id_type=MESH)
    )
    loads = [
        pltpu.make_async_copy(src, dst, load_sem.at[n])
        for n, (src, dst) in enumerate(((fb_hbm, fb), (fv_hbm, fv), (cb_hbm, cb), (cv_hbm, cv)))
    ]
    listed = pltpu.make_async_copy(pairs_hbm, pairs, load_sem.at[4])
    listed.start()
    for load in loads:
        load.start()
    each_group(
        lambda g: pl.semaphore_signal(barrier, inc=1, device_id=(me, g), device_id_type=MESH)
    )

    lane = lax.broadcasted_iota(jnp.int32, (ROWS, LANES), 1)
    sub = lax.broadcasted_iota(jnp.int32, (ROWS, LANES), 0)
    zero = jnp.zeros((ROWS, LANES), jnp.float32)
    row16 = lane // EDGE
    k_of = lane % EDGE
    k8 = lane % HALF
    first_y = lane < EDGE
    last_y = lane >= LANES - EDGE
    first_z = k_of == 0
    last_z = k_of == EDGE - 1
    first_x = sub == 0
    last_x = sub == ROWS - 1

    def roll(v, shift):
        return v if shift % LANES == 0 else pltpu.roll(v, shift % LANES, 1)

    def back_y(pair):
        low, high = roll(pair[0], EDGE), roll(pair[1], EDGE)
        return jnp.where(first_y, high, low), jnp.where(first_y, low, high)

    def ahead_y(pair):
        low, high = roll(pair[0], -EDGE), roll(pair[1], -EDGE)
        return jnp.where(last_y, high, low), jnp.where(last_y, low, high)

    def back_z(pair):
        return tuple(jnp.where(first_z, roll(v, 1 - EDGE), roll(v, 1)) for v in pair)

    def ahead_z(pair):
        return tuple(jnp.where(last_z, roll(v, EDGE - 1), roll(v, -1)) for v in pair)

    def add(a, b):
        return tuple(x + y for x, y in zip(a, b))

    def sub2(a, b):
        return tuple(x - y for x, y in zip(a, b))

    def mul(a, b):
        return tuple(x * y for x, y in zip(a, b))

    def quad(f):
        return lambda q: f(q[:2]) + f(q[2:])

    def back_x(q):
        r = [pltpu.roll(v, 1, 0) for v in q]
        return tuple(jnp.where(first_x, r[n ^ 2], r[n]) for n in range(4))

    def ahead_x(q):
        r = [pltpu.roll(v, ROWS - 1, 0) for v in q]
        return tuple(jnp.where(last_x, r[n ^ 2], r[n]) for n in range(4))

    def top_of(v, c):
        out = []
        for n in range(len(v[0])):
            vv = (v[0][n] * v[0][n] + v[1][n] * v[1][n]) + v[2][n] * v[2][n]
            cc = (c[0][n] * c[0][n] + c[1][n] * c[1][n]) + c[2][n] * c[2][n]
            root_v = vv * lax.rsqrt(jnp.maximum(vv, TINY))
            root_c = cc * lax.rsqrt(jnp.maximum(cc, TINY))
            out.append(root_v + 0.5 * root_c)
        return functools.reduce(jnp.maximum, out)

    def cells(v, c):
        return (
            sub2(mul(v[2], c[1]), mul(v[1], c[2])),
            sub2(mul(v[0], c[2]), mul(v[2], c[0])),
            sub2(mul(v[1], c[0]), mul(v[0], c[1])),
        )

    def fine_read(ref, base):
        return tuple(
            tuple(
                ref[pl.ds(base + c * TILES + 2 * HALF * ih + h, ROWS, stride=2), :]
                for ih in range(2)
                for h in range(2)
            )
            for c in range(3)
        )

    def fine_put(ref, base, values):
        for c in range(3):
            for ih in range(2):
                for h in range(2):
                    ref[pl.ds(base + c * TILES + 2 * HALF * ih + h, ROWS, stride=2), :] = values[c][
                        2 * ih + h
                    ]

    def fine_edges(b, v):
        c = (add(b[0], ahead_x(b[0])), add(b[1], quad(ahead_y)(b[1])), add(b[2], quad(ahead_z)(b[2])))
        cell = cells(v, c)
        part_x = add(cell[0], quad(back_y)(cell[0]))
        part_y = add(cell[1], quad(back_z)(cell[1]))
        part_z = add(cell[2], quad(back_y)(cell[2]))
        e = (
            add(part_x, quad(back_z)(part_x)),
            add(part_y, back_x(part_y)),
            add(part_z, back_x(part_z)),
        )
        return e, c

    def fine_curl(e):
        return (
            sub2(sub2(quad(ahead_y)(e[2]), e[2]), sub2(quad(ahead_z)(e[1]), e[1])),
            sub2(sub2(quad(ahead_z)(e[0]), e[0]), sub2(ahead_x(e[2]), e[2])),
            sub2(sub2(ahead_x(e[1]), e[1]), sub2(quad(ahead_y)(e[0]), e[0])),
        )

    def by_axis(d, values):
        return jnp.where(d == 0, values[0], jnp.where(d == 1, values[1], values[2]))

    def sum_rows(v):
        return jnp.sum(v, axis=0, keepdims=True)

    listed.wait()
    loads[0].wait()
    loads[1].wait()

    half_lane = 32 * (row16 % 4)
    index_r = (half_lane + 2 * k8, 2 * k8, half_lane)
    target_r = (jnp.zeros_like(lane), row16, k8)

    def pair_edges(r):
        base = pairs[r, 0] * SPAN
        fine_put(emf_p, r * SPAN, fine_edges(fine_read(fb, base), fine_read(fv, base))[0])

    def pair_restrict(r):
        d = pairs[r, 1]
        index, target = by_axis(d, index_r), by_axis(d, target_r)
        upper = lane >= jnp.where(d == 1, LANES, 64)
        for which in range(2):
            axis = jnp.where(d == 0, 1, 0) if which == 0 else jnp.where(d == 2, 1, 2)
            base = r * SPAN + axis * TILES
            got = []
            for h in range(2):
                here = emf_p[pl.ds(base + h, ROWS, stride=4), :]
                if which == 0:
                    there = jnp.where(
                        d == 0, roll(here, -EDGE), emf_p[pl.ds(base + h + 2, ROWS, stride=4), :]
                    )
                else:
                    there = jnp.where(d == 2, roll(here, -EDGE), roll(here, -1))
                got.append(take(0.5 * (here + there), index))
            value = jnp.where(upper, got[1], got[0])
            rows1[pl.ds(4 * r + which, 1), :] = sum_rows(jnp.where(sub == target, value, 0.0))
        code = (pairs[r, 3] * 6 + d * 2 + pairs[r, 4]).astype(jnp.float32)
        key = jnp.where((lane[:1] // HALF) % 2 == pairs[r, 5], code, -1.0)
        rows1[pl.ds(4 * r + 2, 1), :] = key

    def each_pair(body):
        if pair_count <= 4:
            for r in range(pair_count):
                body(r)
        else:
            lax.fori_loop(0, pair_count, lambda r, _: (body(r), 0)[1], 0)

    each_pair(pair_edges)
    each_pair(pair_restrict)

    slot_of = [pairs[r, 0] for r in range(pair_count)]
    face_of = [pairs[r, 1] for r in range(pair_count)]
    owner_of = [pairs[r, 2] for r in range(pair_count)]
    rank_of = []
    for r in range(pair_count):
        rank = jnp.int32(0)
        for q in range(r):
            rank = rank + jnp.where(owner_of[q] == owner_of[r], 1, 0)
        rank_of.append(rank)

    def build(p, carry):
        message = jnp.full((ROWS, LANES), -1.0, jnp.float32)
        for r in range(pair_count):
            here = jnp.where(owner_of[r] == p, rank_of[r], ROWS)
            for n, row in enumerate((2 * here, 2 * here + 1, 2 * CAP + here)):
                message = jnp.where(
                    sub == row, jnp.broadcast_to(rows1[4 * r + n : 4 * r + n + 1, :], (ROWS, LANES)), message
                )
        slot(send1, p)[...] = message
        return carry

    def slot(ref, p):
        return ref.at[pl.ds(pl.multiple_of(p * ROWS, ROWS), ROWS)]

    lax.fori_loop(0, peers, build, 0, unroll=few)

    pl.semaphore_wait(barrier, peers - 1 + groups - 1)

    def out1(p):
        return pltpu.make_async_remote_copy(
            src_ref=slot(send1, p), dst_ref=slot(recv1, me), send_sem=s1_sem,
            recv_sem=r1_sem, device_id=(p, mg), device_id_type=MESH,
        )

    def out2(p):
        return pltpu.make_async_remote_copy(
            src_ref=slot(send2, p), dst_ref=slot(recv2, me), send_sem=s2_sem,
            recv_sem=r2_sem, device_id=(p, mg), device_id_type=MESH,
        )

    def outg(g):
        return pltpu.make_async_remote_copy(
            src_ref=gmax, dst_ref=slot(gmax_in, mg), send_sem=sg_sem,
            recv_sem=rg_sem, device_id=(me, g), device_id_type=MESH,
        )

    def drain(ref, sem, count):
        part = ref.at[pl.ds(0, ROWS * count)]
        pltpu.make_async_copy(part, part, sem).wait()

    each_peer(lambda p: out1(p).start())

    loads[2].wait()
    loads[3].wait()

    def column(tile):
        return pl.ds(pl.multiple_of(tile * LANES, LANES), LANES)

    def blocked(ref, g):
        def read(c, i):
            return tuple(ref[c, ROWS * g : ROWS * g + ROWS, column(2 * i + h)] for h in range(2))

        return read

    def blocked_put(ref, g):
        def put(c, i, pair):
            for h in range(2):
                ref[c, ROWS * g : ROWS * g + ROWS, column(2 * i + h)] = pair[h]

        return put


    def coarse_step(n, carry):
        parts, best = carry
        parts = list(parts)
        for u in range(COARSE_STEP):
            i = n * COARSE_STEP + u
            after = lax.rem(i + 1, EDGE)
            for g in range(coarse_groups):
                field, velocity, put = blocked(cb, g), blocked(cv, g), blocked_put(emf_c, g)
                b = [field(c, i) for c in range(3)]
                v = [velocity(c, i) for c in range(3)]
                c = (add(b[0], field(0, after)), add(b[1], ahead_y(b[1])), add(b[2], ahead_z(b[2])))
                cell = cells(v, c)
                part_x = add(cell[0], back_y(cell[0]))
                part_y = add(cell[1], back_z(cell[1]))
                part_z = add(cell[2], back_y(cell[2]))
                put(0, i, add(part_x, back_z(part_x)))
                put(1, i, add(part_y, parts[g][0]))
                put(2, i, add(part_z, parts[g][1]))
                parts[g] = (part_y, part_z)
                best = jnp.maximum(best, top_of(v, c))
        return tuple(parts), best

    nothing = ((zero, zero), (zero, zero))
    parts, best = lax.fori_loop(
        0, EDGE // COARSE_STEP, coarse_step, ((nothing,) * coarse_groups, zero)
    )
    for g in range(coarse_groups):
        read, put = blocked(emf_c, g), blocked_put(emf_c, g)
        for c in range(2):
            put(1 + c, 0, add(read(1 + c, 0), parts[g][c]))

    fine_step = largest_step(fine_count, FINE_STEP)

    def fine_bulk(n, best):
        for u in range(fine_step):
            base = (n * fine_step + u) * SPAN
            b, v = fine_read(fb, base), fine_read(fv, base)
            e, c = fine_edges(b, v)
            fine_put(curl_f, base, fine_curl(e))
            best = jnp.maximum(best, top_of(v, c))
        return best

    best = lax.fori_loop(0, fine_count // fine_step, fine_bulk, best)
    gmax[...] = best
    each_group(lambda g: outg(g).start())


    def packed(read, c, d, q1):
        if d == 0:
            return read(c, 0)[q1]
        out = zero
        for m in range(HALF):
            tiles = read(c, q1 * HALF + m)
            if d == 1:
                out = jnp.where(row16 == m, roll(tiles[0], EDGE * m), out)
            else:
                for q2 in range(2):
                    out = jnp.where(k_of == HALF * q2 + m, roll(tiles[q2], HALF * q2 + m), out)
        return out

    def plane_slot(n, g):
        at = (n * coarse_groups + g) * ROWS
        return slice(at, at + ROWS)

    for g in range(coarse_groups):
        for d in range(3):
            for q1 in range(2):
                plane_b[plane_slot(2 * d + q1, g), :] = packed(blocked(cb, g), d, d, q1)
                for which in range(2):
                    plane_e[plane_slot(4 * d + 2 * which + q1, g), :] = packed(
                        blocked(emf_c, g), TANGENT[d][which], d, q1
                    )

    def row_of(ref, n):
        return jnp.broadcast_to(ref[pl.ds(n, 1), :], (ROWS, LANES))

    slot(recv1, me)[...] = slot(send1, me)[...]
    drain(recv1, r1_sem, peers - 1)

    base_code = [((sub + ROWS * g) * 6).astype(jnp.float32) for g in range(coarse_groups)]
    empty = jnp.full((ROWS, LANES), EMPTY, jnp.float32)
    for g in range(coarse_groups):

        def collect(p, held, g=g):
            for c in range(CAP):
                code = row_of(recv1, p * ROWS + 2 * CAP + c) - base_code[g]
                values = [row_of(recv1, p * ROWS + 2 * c + which) for which in range(2)]
                held = [
                    jnp.where(code == float(2 * (n // 4) + n % 2), values[n // 2 % 2], held[n])
                    for n in range(12)
                ]
            return held

        held = lax.fori_loop(0, peers, collect, [empty] * 12, unroll=few)
        for n in range(12):
            held_ref[plane_slot(n, g), :] = held[n]

    spread = row16
    squeeze = EDGE * k8

    def ahead_i(pair):
        turned = [roll(v, -1) for v in pair]
        wrapped = [roll(v, HALF - 1) for v in pair]
        return tuple(jnp.where(k8 == HALF - 1, wrapped[1 - q], turned[q]) for q in range(2))

    def ahead_j(pair):
        return tuple(
            jnp.where(
                last_y,
                jnp.where(k_of < HALF, roll(v, LANES - EDGE - HALF), roll(v, LANES - HALF)),
                roll(v, -EDGE),
            )
            for v in pair
        )

    for g in range(coarse_groups):
        hold = [held_ref[plane_slot(n, g), :] for n in range(12)]
        sent = [[(hold[4 * d + 2 * w], hold[4 * d + 2 * w + 1]) for w in range(2)] for d in range(3)]
        now = [
            [
                [
                    jnp.where(
                        sent[d][w][q] < BIG, sent[d][w][q], plane_e[plane_slot(4 * d + 2 * w + q, g), :]
                    )
                    for q in range(2)
                ]
                for w in range(2)
            ]
            for d in range(3)
        ]
        for q in range(2):
            over = take(sent[2][0][q], spread)
            now[1][0][q] = jnp.where((over < BIG) & first_z, over, now[1][0][q])
            under = take(sent[1][0][q], squeeze)
            free = (sent[2][0][q] >= BIG) & (lane < HALF) & (under < BIG)
            now[2][0][q] = jnp.where(free, under, now[2][0][q])
            over = roll(sent[2][1][0], -HALF * q)
            now[0][0][q] = jnp.where((over < BIG) & first_z, over, now[0][0][q])
            under = roll(sent[0][0][q], HALF * q)
            free = (sent[2][1][0] >= BIG) & (k_of == HALF * q) & (under < BIG)
            now[2][1][0] = jnp.where(free, under, now[2][1][0])
        over, under = sent[1][1][0], sent[0][1][0]
        now[0][1][0] = jnp.where((over < BIG) & first_y, over, now[0][1][0])
        now[1][1][0] = jnp.where((over >= BIG) & first_y & (under < BIG), under, now[1][1][0])
        for d in range(3):
            one, two = now[d]
            if d < 2:
                ahead_one, ahead_two = ahead_y(two), ahead_z(one)
            else:
                ahead_one, ahead_two = ahead_i(two), ahead_j(one)
            left, right = sub2(ahead_one, two), sub2(ahead_two, one)
            curl = sub2(right, left) if d == 1 else sub2(left, right)
            for q in range(2):
                plane_n[plane_slot(2 * d + q, g), :] = curl[q]

    drain(gmax_in, rg_sem, groups - 1)
    for k in range(1, groups):
        best = jnp.maximum(best, slot(gmax_in, lax.rem(mg + k, groups))[...])
    top_row = jnp.broadcast_to(jnp.max(best, axis=0, keepdims=True), (ROWS, LANES))

    def answer(p, carry):
        rows = top_row
        for c in range(CAP):
            key = row_of(recv1, p * ROWS + 2 * CAP + c)
            curl_acc, field_acc = zero, zero
            for g in range(coarse_groups):
                code = key - base_code[g]
                for n in range(6):
                    hit = code == float(n)
                    curl_acc = jnp.where(hit, plane_n[plane_slot(n, g), :], curl_acc)
                    field_acc = jnp.where(hit, plane_b[plane_slot(n, g), :], field_acc)
            rows = jnp.where(sub == c, sum_rows(curl_acc), rows)
            rows = jnp.where(sub == CAP + c, sum_rows(field_acc), rows)
        slot(send2, p)[...] = rows
        return carry

    lax.fori_loop(0, peers, answer, 0, unroll=few)
    each_peer(lambda p: out2(p).start())

    for g in range(coarse_groups):
        for d in range(3):
            for which in range(2):
                axis = TANGENT[d][which]
                for q1 in range(2):
                    value = held_ref[plane_slot(4 * d + 2 * which + q1, g), :]

                    def patch(tile, shift, mask, value=value, axis=axis, g=g):
                        where = (axis, slice(ROWS * g, ROWS * g + ROWS), slice(tile * LANES, tile * LANES + LANES))
                        turned = roll(value, shift)
                        put = turned < BIG
                        if mask is not None:
                            put = put & mask
                        emf_c[where] = jnp.where(put, turned, emf_c[where])

                    if d == 0:
                        patch(q1, 0, None)
                        continue
                    for m in range(HALF):
                        tile = 2 * (q1 * HALF + m)
                        if d == 1:
                            patch(tile, -EDGE * m, first_y)
                        else:
                            for q2 in range(2):
                                patch(tile + q2, -(HALF * q2 + m), first_z)


    def curl_step(n, carry):
        for u in range(4):
            i = 4 * n + u
            after = lax.rem(i + 1, EDGE)
            for g in range(coarse_groups):
                read, put = blocked(emf_c, g), blocked_put(curl_c, g)
                e_x, e_y, e_z = read(0, i), read(1, i), read(2, i)
                put(0, i, sub2(sub2(ahead_y(e_z), e_z), sub2(ahead_z(e_y), e_y)))
                put(1, i, sub2(sub2(ahead_z(e_x), e_x), sub2(read(2, after), e_z)))
                put(2, i, sub2(sub2(read(1, after), e_y), sub2(ahead_y(e_x), e_x)))
        return carry

    lax.fori_loop(0, EDGE // 4, curl_step, 0)

    index_n = (lane, k_of, EDGE * k8)
    target_n = (jnp.zeros_like(lane), row16, row16)

    def pair_normal(r):
        d = pairs[r, 1]
        base = pairs[r, 0] * SPAN + d * TILES
        index, target = by_axis(d, index_n), by_axis(d, target_n)
        upper = k_of >= jnp.where(d == 2, HALF, EDGE)
        for n, ref in enumerate((fb, curl_f)):
            for h in range(2):
                start = base + jnp.where(d == 0, h, 2 * HALF * h)
                got = [take(ref[pl.ds(start + s, ROWS, stride=2), :], index) for s in range(2)]
                value = jnp.where(upper, got[1], got[0])
                picked[pl.ds((2 * n + h) * pair_rows + r, 1), :] = sum_rows(
                    jnp.where(sub == target, value, 0.0)
                )

    each_pair(pair_normal)

    slot(recv2, me)[...] = slot(send2, me)[...]
    drain(recv2, r2_sem, peers - 1)
    top = lax.fori_loop(
        0, peers, lambda p, t: jnp.maximum(t, row_of(recv2, p * ROWS + 2 * CAP)), zero, unroll=few
    )
    step_out[...] = jnp.broadcast_to(0.125 * (0.2 / jnp.max(top, axis=1, keepdims=True)), (ROWS, LANES))
    for r in range(pair_count):
        row = owner_of[r] * ROWS + rank_of[r]
        own_a[r : r + 1, :] = recv2[pl.ds(row, 1), :]
        own_b[r : r + 1, :] = recv2[pl.ds(row + CAP, 1), :]
    for s in range(0, pair_count, ROWS):
        turned, column_of = jnp.zeros_like(lane), jnp.zeros_like(lane)
        for r in range(s, min(s + ROWS, pair_count)):
            turned = jnp.where(sub == r - s, face_of[r], turned)
            column_of = jnp.where(sub == r - s, pairs[r, 5], column_of)
        for h in range(2):
            m, n = 4 * h + lane // 32, k_of // 2
            index = jnp.where(turned == 2, EDGE * n + m, EDGE * m + n) + HALF * column_of
            curl, field = take(own_a[s : s + ROWS, :], index), take(own_b[s : s + ROWS, :], index)
            side = slice(h * LANES, (h + 1) * LANES)
            fine = [picked[n * pair_rows + s : n * pair_rows + s + ROWS, :] for n in (h, 2 + h)]
            jump_a[s : s + ROWS, side] = fine[0] - field
            jump_b[s : s + ROWS, side] = 2.0 * fine[1] - curl
    drain(send1, s1_sem, peers - 1)
    drain(send2, s2_sem, peers - 1)
    drain(gmax_in, sg_sem, groups - 1)


def store(cb, curl_c, fb, curl_f, jump_a, jump_b, step, out_c, out_f, out_j, new_c, new_f, new_j, sems):
    by = step[0:1, 0:1]
    copies = []
    for c in range(3):
        new_c[c] = cb[c] - by * curl_c[c]
        copies.append(pltpu.make_async_copy(new_c.at[c], out_c.at[c], sems.at[len(copies)]))
        copies[-1].start()
    rows = fb.shape[0]
    for n in range(2):
        part = pl.ds(n * (rows // 2), rows // 2)
        new_f[part, :] = fb[part, :] - (2.0 * by) * curl_f[part, :]
        copies.append(pltpu.make_async_copy(new_f.at[part], out_f.at[part], sems.at[len(copies)]))
        copies[-1].start()
    count = out_j.shape[0]
    new_j[...] = (jump_a[...] - by * jump_b[...])[:count]
    copies.append(pltpu.make_async_copy(new_j, out_j, sems.at[len(copies)]))
    copies[-1].start()
    for copy in copies:
        copy.wait()


def on_device(peers, groups, coarse_field, coarse_velocity, fine_field, fine_velocity, pairs):
    coarse_count, fine_count = coarse_field.shape[1], fine_field.shape[1]
    pair_count = pairs.shape[1]
    cells = EDGE**3
    flat_rows = fine_count * SPAN

    def coarse_view(x):
        return jnp.transpose(x[0], (1, 0, 2))

    def fine_view(x):
        return x.reshape(flat_rows, LANES)

    pair_rows = ROWS * -(-pair_count // ROWS)
    operands = [
        pltpu.with_memory_space_constraint(x, pltpu.HBM)
        for x in (
            pairs[0],
            coarse_view(coarse_field),
            coarse_view(coarse_velocity),
            fine_view(fine_field),
            fine_view(fine_velocity),
        )
    ]
    f32 = jnp.float32
    dma = pltpu.SemaphoreType.DMA
    vmem = pltpu.VMEM
    anywhere = pl.BlockSpec(memory_space=pltpu.HBM)
    inside = pl.BlockSpec(memory_space=pltpu.VMEM)
    coarse_shape, fine_shape = (3, coarse_count, cells), (flat_rows, LANES)
    shapes = (
        coarse_shape,
        coarse_shape,
        fine_shape,
        fine_shape,
        (pair_rows, EDGE * EDGE),
        (pair_rows, EDGE * EDGE),
        (ROWS, LANES),
    )
    results = pl.pallas_call(
        functools.partial(kernel, peers, groups, coarse_count, fine_count, pair_count),
        out_shape=tuple(jax.ShapeDtypeStruct(s, f32) for s in shapes),
        in_specs=[anywhere] * 5,
        out_specs=(inside,) * len(shapes),
        scratch_shapes=[
            pltpu.SMEM(pairs.shape[1:], jnp.int32),
            vmem(coarse_shape, f32),
            vmem(fine_shape, f32),
            vmem(coarse_shape, f32),
            vmem((pair_count * SPAN, LANES), f32),
            vmem((12 * coarse_count, LANES), f32),
            vmem((6 * coarse_count, LANES), f32),
            vmem((6 * coarse_count, LANES), f32),
            vmem((12 * coarse_count, LANES), f32),
            vmem((pair_rows, LANES), f32),
            vmem((pair_rows, LANES), f32),
            vmem((4 * pair_rows, LANES), f32),
            vmem((4 * pair_rows, LANES), f32),
            vmem((peers * ROWS, LANES), f32),
            vmem((peers * ROWS, LANES), f32),
            vmem((peers * ROWS, LANES), f32),
            vmem((peers * ROWS, LANES), f32),
            vmem((ROWS, LANES), f32),
            vmem((groups * ROWS, LANES), f32),
            dma((5,)),
            dma,
            dma,
            dma,
            dma,
            dma,
            dma,
        ],
        compiler_params=pltpu.CompilerParams(
            collective_id=0, has_side_effects=True, vmem_limit_bytes=32 * 1024 * 1024
        ),
    )(*operands)
    coarse_out, fine_out, jump = pl.pallas_call(
        store,
        out_shape=(
            jax.ShapeDtypeStruct(coarse_shape, f32),
            jax.ShapeDtypeStruct(fine_shape, f32),
            jax.ShapeDtypeStruct((pair_count, EDGE * EDGE), f32),
        ),
        in_specs=[inside] * len(shapes),
        out_specs=(anywhere,) * 3,
        scratch_shapes=[
            vmem(coarse_shape, f32),
            vmem(fine_shape, f32),
            vmem((pair_count, EDGE * EDGE), f32),
            dma((6,)),
        ],
    )(*(pltpu.with_memory_space_constraint(x, pltpu.VMEM) for x in results))
    return (
        jnp.transpose(coarse_out, (1, 0, 2))[None],
        fine_out.reshape(1, fine_count, 3, cells),
        jump[None],
    )


def solution(mesh):
    spec = P("gz", "blocks", None, None)
    flat = P("gz", "blocks", None)
    return jax.shard_map(
        functools.partial(on_device, mesh.shape["blocks"], mesh.shape["gz"]),
        mesh=mesh,
        in_specs=(spec, spec, spec, spec, flat),
        out_specs=(spec, spec, flat),
        check_vma=False,
    )
```

time: 27.4 us -> 18 us (0.66)
  Pallas kernels: 26.6 us -> 17.1 us
    pallas_call x1, Pallas kernels: 25.5 us -> 15.9 us  [on_device(): pl.pallas_call(functools.partial(kernel, peers, groups, coarse_count, fin...]
where the time goes in v1:
time: 18 us; the launch traced here: 17.8 us
  Pallas kernels  17.1 us (95%)
  between operations  0.64 us (4%)
    pallas_call x1, Pallas kernels, on_device(): pl.pallas_call(functools.partial(kernel, peers, groups, coarse_count, fin...  15.9 us
    pallas_call x1, Pallas kernels, on_device(): pl.pallas_call(store, out_shape=(jax.ShapeDtypeStruct(coarse_shape, f32),...  1.2 us

profile of v1, /device:TPU:0, one launch (start us, length us, event | category | flops | bytes accessed | tf_op | source)
XLA Modules:
  0.0 17.8 jit_solution(15068570457649667045)
XLA Ops:
  0.6 15.9 %shard_map.76 = (f32[3,16,4096]{2,1,0:T(8,128)S(1)}, f32[3,16,4096]{2,1,0:T(8,128)S(1)}, f32[1152,128]{1,0:T(8,128)S(1)}, f32[1152,128]{1,0:T(8,128)S(1)}, f32[8...) custom-call(s32[4,6]{1,0:T(4,128)} %bitcast.18, f32[3,16,4096]{2,1,0:T(8,128)} %bitcast.14, ...), custom_call_target="tpu_custom_call" | custom-call | tf_op jit(solution)/shard_map/pallas_call | solution.py:662
  16.6 1.2 %shard_map.77 = (f32[3,16,4096]{2,1,0:T(8,128)}, f32[1152,128]{1,0:T(8,128)}, f32[4,256]{1,0:T(4,128)}) custom-call(f32[3,16,4096]{2,1,0:T(8,128)S(1)} %get-tuple-element.13.cb, f32[3,16,4096]{2,1,0:T(8,128)S(1)} %get-tuple-element.14.curl_c, f32[1152,128]{1,0:T(8,128)S(1)} %get-tuple-element.15.fb, f32[1152,128]{1,0:T(8,128)S(1)} %get-tuple-element.16.curl_f, ...), custom_call_target="tpu_custom_call" | custom-call | tf_op jit(solution)/shard_map/pallas_call | solution.py:699

commit v2 on v1

--- a/solution.py
+++ b/solution.py
@@ -19,8 +19,10 @@
 EMPTY = 3e38
 TANGENT = ((1, 2), (0, 2), (0, 1))
 MESH = pl.DeviceIdType.MESH
-COARSE_STEP = 8
+CHUNK = 4
+CHUNKS = EDGE // CHUNK
 FINE_STEP = 4
+SPEED_STEP = 6
 
 
 def take(values, index):
@@ -54,6 +56,8 @@
     fv,
     emf_c,
     emf_p,
+    centred,
+    halfway,
     plane_e,
     plane_b,
     plane_n,
@@ -190,18 +194,19 @@
                         2 * ih + h
                     ]
 
+    def fine_centre(b):
+        return (add(b[0], ahead_x(b[0])), add(b[1], quad(ahead_y)(b[1])), add(b[2], quad(ahead_z)(b[2])))
+
     def fine_edges(b, v):
-        c = (add(b[0], ahead_x(b[0])), add(b[1], quad(ahead_y)(b[1])), add(b[2], quad(ahead_z)(b[2])))
-        cell = cells(v, c)
+        cell = cells(v, fine_centre(b))
         part_x = add(cell[0], quad(back_y)(cell[0]))
         part_y = add(cell[1], quad(back_z)(cell[1]))
         part_z = add(cell[2], quad(back_y)(cell[2]))
-        e = (
+        return (
             add(part_x, quad(back_z)(part_x)),
             add(part_y, back_x(part_y)),
             add(part_z, back_x(part_z)),
         )
-        return e, c
 
     def fine_curl(e):
         return (
@@ -226,7 +231,7 @@
 
     def pair_edges(r):
         base = pairs[r, 0] * SPAN
-        fine_put(emf_p, r * SPAN, fine_edges(fine_read(fb, base), fine_read(fv, base))[0])
+        fine_put(emf_p, r * SPAN, fine_edges(fine_read(fb, base), fine_read(fv, base)))
 
     def pair_restrict(r):
         d = pairs[r, 1]
@@ -287,6 +292,98 @@
 
     lax.fori_loop(0, peers, build, 0, unroll=few)
 
+    loads[2].wait()
+    loads[3].wait()
+
+    def column(tile):
+        return pl.ds(pl.multiple_of(tile * LANES, LANES), LANES)
+
+    def blocked(ref, g):
+        def read(c, i):
+            return tuple(ref[c, ROWS * g : ROWS * g + ROWS, column(2 * i + h)] for h in range(2))
+
+        return read
+
+    def blocked_put(ref, g):
+        def put(c, i, pair):
+            for h in range(2):
+                ref[c, ROWS * g : ROWS * g + ROWS, column(2 * i + h)] = pair[h]
+
+        return put
+
+
+    def at(n, u, g, h):
+        return pl.ds((((n * CHUNK + u) * coarse_groups + g) * 2 + h) * ROWS, ROWS)
+
+    def each_plane(body):
+        for u in range(CHUNK):
+            for g in range(coarse_groups):
+                body(u, g)
+
+    def centre(chunk):
+        def plane(u, g):
+            i = chunk * CHUNK + u
+            field = blocked(cb, g)
+            b = [field(c, i) for c in range(3)]
+            c = (
+                add(b[0], field(0, lax.rem(i + 1, EDGE))),
+                add(b[1], ahead_y(b[1])),
+                add(b[2], ahead_z(b[2])),
+            )
+            for n in range(3):
+                for h in range(2):
+                    centred[at(n, u, g, h), :] = c[n][h]
+
+        each_plane(plane)
+
+    def coarse_step(t, carry):
+        parts, best = carry
+        parts = list(parts)
+
+        def last(u, g):
+            part_x = tuple(halfway[at(0, u, g, h), :] for h in range(2))
+            i = lax.rem(t + CHUNKS - 2, CHUNKS) * CHUNK + u
+            blocked_put(emf_c, g)(0, i, add(part_x, back_z(part_x)))
+
+        each_plane(last)
+        tops = []
+
+        def middle(u, g):
+            i = lax.rem(t + CHUNKS - 1, CHUNKS) * CHUNK + u
+            put = blocked_put(emf_c, g)
+            c = [tuple(centred[at(n, u, g, h), :] for h in range(2)) for n in range(3)]
+            v = [blocked(cv, g)(n, i) for n in range(3)]
+            cell = cells(v, c)
+            part_x = add(cell[0], back_y(cell[0]))
+            part_y = add(cell[1], back_z(cell[1]))
+            part_z = add(cell[2], back_y(cell[2]))
+            for h in range(2):
+                halfway[at(0, u, g, h), :] = part_x[h]
+            put(1, i, add(part_y, parts[g][0]))
+            put(2, i, add(part_z, parts[g][1]))
+            parts[g] = (part_y, part_z)
+            tops.append(top_of(v, c))
+
+        each_plane(middle)
+        centre(lax.rem(t, CHUNKS))
+        return tuple(parts), functools.reduce(jnp.maximum, tops, best)
+
+    centre(CHUNKS - 1)
+    nothing = ((zero, zero), (zero, zero))
+    best = lax.fori_loop(0, CHUNKS + 2, coarse_step, ((nothing,) * coarse_groups, zero))[1]
+
+    speed_step = largest_step(fine_count, SPEED_STEP)
+
+    def fine_top(n, best):
+        for u in range(speed_step):
+            base = (n * speed_step + u) * SPAN
+            b, v = fine_read(fb, base), fine_read(fv, base)
+            best = jnp.maximum(best, top_of(v, fine_centre(b)))
+        return best
+
+    best = lax.fori_loop(0, fine_count // speed_step, fine_top, best)
+    gmax[...] = best
+
     pl.semaphore_wait(barrier, peers - 1 + groups - 1)
 
     def out1(p):
@@ -311,73 +408,18 @@
         part = ref.at[pl.ds(0, ROWS * count)]
         pltpu.make_async_copy(part, part, sem).wait()
 
+    each_group(lambda g: outg(g).start())
     each_peer(lambda p: out1(p).start())
 
-    loads[2].wait()
-    loads[3].wait()
-
-    def column(tile):
-        return pl.ds(pl.multiple_of(tile * LANES, LANES), LANES)
-
-    def blocked(ref, g):
-        def read(c, i):
-            return tuple(ref[c, ROWS * g : ROWS * g + ROWS, column(2 * i + h)] for h in range(2))
-
-        return read
-
-    def blocked_put(ref, g):
-        def put(c, i, pair):
-            for h in range(2):
-                ref[c, ROWS * g : ROWS * g + ROWS, column(2 * i + h)] = pair[h]
-
-        return put
-
-
-    def coarse_step(n, carry):
-        parts, best = carry
-        parts = list(parts)
-        for u in range(COARSE_STEP):
-            i = n * COARSE_STEP + u
-            after = lax.rem(i + 1, EDGE)
-            for g in range(coarse_groups):
-                field, velocity, put = blocked(cb, g), blocked(cv, g), blocked_put(emf_c, g)
-                b = [field(c, i) for c in range(3)]
-                v = [velocity(c, i) for c in range(3)]
-                c = (add(b[0], field(0, after)), add(b[1], ahead_y(b[1])), add(b[2], ahead_z(b[2])))
-                cell = cells(v, c)
-                part_x = add(cell[0], back_y(cell[0]))
-                part_y = add(cell[1], back_z(cell[1]))
-                part_z = add(cell[2], back_y(cell[2]))
-                put(0, i, add(part_x, back_z(part_x)))
-                put(1, i, add(part_y, parts[g][0]))
-                put(2, i, add(part_z, parts[g][1]))
-                parts[g] = (part_y, part_z)
-                best = jnp.maximum(best, top_of(v, c))
-        return tuple(parts), best
-
-    nothing = ((zero, zero), (zero, zero))
-    parts, best = lax.fori_loop(
-        0, EDGE // COARSE_STEP, coarse_step, ((nothing,) * coarse_groups, zero)
-    )
-    for g in range(coarse_groups):
-        read, put = blocked(emf_c, g), blocked_put(emf_c, g)
-        for c in range(2):
-            put(1 + c, 0, add(read(1 + c, 0), parts[g][c]))
-
     fine_step = largest_step(fine_count, FINE_STEP)
 
-    def fine_bulk(n, best):
+    def fine_bulk(n, carry):
         for u in range(fine_step):
             base = (n * fine_step + u) * SPAN
-            b, v = fine_read(fb, base), fine_read(fv, base)
-            e, c = fine_edges(b, v)
-            fine_put(curl_f, base, fine_curl(e))
-            best = jnp.maximum(best, top_of(v, c))
-        return best
-
-    best = lax.fori_loop(0, fine_count // fine_step, fine_bulk, best)
-    gmax[...] = best
-    each_group(lambda g: outg(g).start())
+            fine_put(curl_f, base, fine_curl(fine_edges(fine_read(fb, base), fine_read(fv, base))))
+        return carry
+
+    lax.fori_loop(0, fine_count // fine_step, fine_bulk, 0)
 
 
     def packed(read, c, d, q1):
@@ -670,6 +712,8 @@
             vmem(fine_shape, f32),
             vmem(coarse_shape, f32),
             vmem((pair_count * SPAN, LANES), f32),
+            vmem((6 * CHUNK * coarse_count, LANES), f32),
+            vmem((2 * CHUNK * coarse_count, LANES), f32),
             vmem((12 * coarse_count, LANES), f32),
             vmem((6 * coarse_count, LANES), f32),
             vmem((6 * coarse_count, LANES), f32),

time: 18 us -> 16.7 us (0.928)
  Pallas kernels: 17.1 us -> 15.9 us
    pallas_call x1, Pallas kernels: 15.9 us -> 14.7 us  [on_device(): pl.pallas_call(functools.partial(kernel, peers, groups, coarse_count, fin...]
where the time goes in v2:
time: 16.7 us; the launch traced here: 16.6 us
  Pallas kernels  15.9 us (95%)
  between operations  0.64 us (4%)
    pallas_call x1, Pallas kernels, on_device(): pl.pallas_call(functools.partial(kernel, peers, groups, coarse_count, fin...  14.7 us
    pallas_call x1, Pallas kernels, on_device(): pl.pallas_call(store, out_shape=(jax.ShapeDtypeStruct(coarse_shape, f32),...  1.2 us

profile of v2, /device:TPU:0, one launch (start us, length us, event | category | flops | bytes accessed | tf_op | source)
XLA Modules:
  0.0 16.6 jit_solution(3200174102123204737)
XLA Ops:
  0.6 14.7 %shard_map.76 = (f32[3,16,4096]{2,1,0:T(8,128)S(1)}, f32[3,16,4096]{2,1,0:T(8,128)S(1)}, f32[1152,128]{1,0:T(8,128)S(1)}, f32[1152,128]{1,0:T(8,128)S(1)}, f32[8...) custom-call(s32[4,6]{1,0:T(4,128)} %bitcast.18, f32[3,16,4096]{2,1,0:T(8,128)} %bitcast.14, ...), custom_call_target="tpu_custom_call" | custom-call | tf_op jit(solution)/shard_map/pallas_call | solution.py:704
  15.4 1.2 %shard_map.77 = (f32[3,16,4096]{2,1,0:T(8,128)}, f32[1152,128]{1,0:T(8,128)}, f32[4,256]{1,0:T(4,128)}) custom-call(f32[3,16,4096]{2,1,0:T(8,128)S(1)} %get-tuple-element.13.cb, f32[3,16,4096]{2,1,0:T(8,128)S(1)} %get-tuple-element.14.curl_c, f32[1152,128]{1,0:T(8,128)S(1)} %get-tuple-element.15.fb, f32[1152,128]{1,0:T(8,128)S(1)} %get-tuple-element.16.curl_f, ...), custom_call_target="tpu_custom_call" | custom-call | tf_op jit(solution)/shard_map/pallas_call | solution.py:743

commit v3 on v2

--- a/solution.py
+++ b/solution.py
@@ -19,6 +19,7 @@
 EMPTY = 3e38
 TANGENT = ((1, 2), (0, 2), (0, 1))
 MESH = pl.DeviceIdType.MESH
+TOP_CHUNK = 4
 CHUNK = 4
 CHUNKS = EDGE // CHUNK
 FINE_STEP = 4
@@ -48,8 +49,10 @@
     curl_c,
     fb,
     curl_f,
-    jump_a,
-    jump_b,
+    picked,
+    own_a,
+    own_b,
+    index_out,
     step_out,
     pairs,
     cv,
@@ -62,9 +65,7 @@
     plane_b,
     plane_n,
     held_ref,
-    own_a,
-    own_b,
-    picked,
+    top_rows,
     rows1,
     send1,
     recv1,
@@ -86,8 +87,28 @@
     coarse_groups = coarse_count // ROWS
     pair_rows = ROWS * -(-pair_count // ROWS)
 
+    paired = peers & (peers - 1) == 0
+    bits = [1 << n for n in range(peers.bit_length() - 1)]
+
+    def target(k):
+        if not paired:
+            return lax.rem(me + k, peers)
+        p = me
+        for bit in bits:
+            p = p + lax.rem(k // bit, 2) * bit * (1 - 2 * lax.rem(me // bit, 2))
+        return p
+
+    def source(k):
+        return target(k) if paired else lax.rem(me + peers - k, peers)
+
+    def each_step(first, last, body, carry=0):
+        def step(n, carry):
+            return body(last - 1 - n, carry)
+
+        return lax.fori_loop(0, last - first, step, carry, unroll=few)
+
     def each_peer(body):
-        lax.fori_loop(1, peers, lambda k, _: (body(lax.rem(me + k, peers)), 0)[1], 0, unroll=few)
+        each_step(1, peers, lambda k, _: (body(target(k)), 0)[1])
 
     def each_group(body):
         for k in range(1, groups):
@@ -292,9 +313,6 @@
 
     lax.fori_loop(0, peers, build, 0, unroll=few)
 
-    loads[2].wait()
-    loads[3].wait()
-
     def column(tile):
         return pl.ds(pl.multiple_of(tile * LANES, LANES), LANES)
 
@@ -311,18 +329,34 @@
 
         return put
 
-
-    def at(n, u, g, h):
-        return pl.ds((((n * CHUNK + u) * coarse_groups + g) * 2 + h) * ROWS, ROWS)
-
-    def each_plane(body):
-        for u in range(CHUNK):
+    speed_step = largest_step(fine_count, SPEED_STEP)
+
+    def fine_top(n, best):
+        for u in range(speed_step):
+            base = (n * speed_step + u) * SPAN
+            b, v = fine_read(fb, base), fine_read(fv, base)
+            best = jnp.maximum(best, top_of(v, fine_centre(b)))
+        return best
+
+    best = lax.fori_loop(0, fine_count // speed_step, fine_top, zero)
+
+    loads[2].wait()
+    loads[3].wait()
+
+
+    def at(n, i, g, h):
+        row = (((n * coarse_groups + g) * EDGE + i) * 2 + h) * ROWS
+        return pl.ds(row if isinstance(row, int) else pl.multiple_of(row, ROWS), ROWS)
+
+    def each_plane(chunk, planes, body):
+        for u in range(planes):
             for g in range(coarse_groups):
-                body(u, g)
-
-    def centre(chunk):
-        def plane(u, g):
-            i = chunk * CHUNK + u
+                body(chunk * planes + u, g)
+
+    def coarse_top(n, best):
+        tops = []
+
+        def plane(i, g):
             field = blocked(cb, g)
             b = [field(c, i) for c in range(3)]
             c = (
@@ -330,66 +364,24 @@
                 add(b[1], ahead_y(b[1])),
                 add(b[2], ahead_z(b[2])),
             )
-            for n in range(3):
+            for k in range(3):
                 for h in range(2):
-                    centred[at(n, u, g, h), :] = c[n][h]
-
-        each_plane(plane)
-
-    def coarse_step(t, carry):
-        parts, best = carry
-        parts = list(parts)
-
-        def last(u, g):
-            part_x = tuple(halfway[at(0, u, g, h), :] for h in range(2))
-            i = lax.rem(t + CHUNKS - 2, CHUNKS) * CHUNK + u
-            blocked_put(emf_c, g)(0, i, add(part_x, back_z(part_x)))
-
-        each_plane(last)
-        tops = []
-
-        def middle(u, g):
-            i = lax.rem(t + CHUNKS - 1, CHUNKS) * CHUNK + u
-            put = blocked_put(emf_c, g)
-            c = [tuple(centred[at(n, u, g, h), :] for h in range(2)) for n in range(3)]
-            v = [blocked(cv, g)(n, i) for n in range(3)]
-            cell = cells(v, c)
-            part_x = add(cell[0], back_y(cell[0]))
-            part_y = add(cell[1], back_z(cell[1]))
-            part_z = add(cell[2], back_y(cell[2]))
-            for h in range(2):
-                halfway[at(0, u, g, h), :] = part_x[h]
-            put(1, i, add(part_y, parts[g][0]))
-            put(2, i, add(part_z, parts[g][1]))
-            parts[g] = (part_y, part_z)
-            tops.append(top_of(v, c))
-
-        each_plane(middle)
-        centre(lax.rem(t, CHUNKS))
-        return tuple(parts), functools.reduce(jnp.maximum, tops, best)
-
-    centre(CHUNKS - 1)
-    nothing = ((zero, zero), (zero, zero))
-    best = lax.fori_loop(0, CHUNKS + 2, coarse_step, ((nothing,) * coarse_groups, zero))[1]
-
-    speed_step = largest_step(fine_count, SPEED_STEP)
-
-    def fine_top(n, best):
-        for u in range(speed_step):
-            base = (n * speed_step + u) * SPAN
-            b, v = fine_read(fb, base), fine_read(fv, base)
-            best = jnp.maximum(best, top_of(v, fine_centre(b)))
-        return best
-
-    best = lax.fori_loop(0, fine_count // speed_step, fine_top, best)
+                    centred[at(k, i, g, h), :] = c[k][h]
+            tops.append(top_of([blocked(cv, g)(k, i) for k in range(3)], c))
+
+        each_plane(n, TOP_CHUNK, plane)
+        return functools.reduce(jnp.maximum, tops, best)
+
+    best = lax.fori_loop(0, EDGE // TOP_CHUNK, coarse_top, best)
     gmax[...] = best
 
     pl.semaphore_wait(barrier, peers - 1 + groups - 1)
 
-    def out1(p):
+    def out1(k):
+        p = target(k)
         return pltpu.make_async_remote_copy(
             src_ref=slot(send1, p), dst_ref=slot(recv1, me), send_sem=s1_sem,
-            recv_sem=r1_sem, device_id=(p, mg), device_id_type=MESH,
+            recv_sem=r1_sem.at[k // (peers - 1)], device_id=(p, mg), device_id_type=MESH,
         )
 
     def out2(p):
@@ -409,17 +401,35 @@
         pltpu.make_async_copy(part, part, sem).wait()
 
     each_group(lambda g: outg(g).start())
-    each_peer(lambda p: out1(p).start())
-
-    fine_step = largest_step(fine_count, FINE_STEP)
-
-    def fine_bulk(n, carry):
-        for u in range(fine_step):
-            base = (n * fine_step + u) * SPAN
-            fine_put(curl_f, base, fine_curl(fine_edges(fine_read(fb, base), fine_read(fv, base))))
-        return carry
-
-    lax.fori_loop(0, fine_count // fine_step, fine_bulk, 0)
+    each_step(1, peers, lambda k, _: (out1(k).start(), 0)[1])
+
+
+    def coarse_step(t, parts):
+        parts = list(parts)
+
+        def last(i, g):
+            part_x = tuple(halfway[at(0, i, g, h), :] for h in range(2))
+            blocked_put(emf_c, g)(0, i, add(part_x, back_z(part_x)))
+
+        def first(i, g):
+            put = blocked_put(emf_c, g)
+            c = [tuple(centred[at(n, i, g, h), :] for h in range(2)) for n in range(3)]
+            cell = cells([blocked(cv, g)(n, i) for n in range(3)], c)
+            part_x = add(cell[0], back_y(cell[0]))
+            part_y = add(cell[1], back_z(cell[1]))
+            part_z = add(cell[2], back_y(cell[2]))
+            for h in range(2):
+                halfway[at(0, i, g, h), :] = part_x[h]
+            put(1, i, add(part_y, parts[g][0]))
+            put(2, i, add(part_z, parts[g][1]))
+            parts[g] = (part_y, part_z)
+
+        each_plane(lax.rem(t + CHUNKS - 1, CHUNKS), CHUNK, last)
+        each_plane(lax.rem(t, CHUNKS), CHUNK, first)
+        return tuple(parts)
+
+    nothing = ((zero, zero), (zero, zero))
+    lax.fori_loop(0, CHUNKS + 1, coarse_step, (nothing,) * coarse_groups)
 
 
     def packed(read, c, d, q1):
@@ -448,95 +458,126 @@
                         blocked(emf_c, g), TANGENT[d][which], d, q1
                     )
 
+    fine_step = largest_step(fine_count, FINE_STEP)
+
+    def fine_bulk(n, carry):
+        for u in range(fine_step):
+            base = (n * fine_step + u) * SPAN
+            fine_put(curl_f, base, fine_curl(fine_edges(fine_read(fb, base), fine_read(fv, base))))
+        return carry
+
+    lax.fori_loop(0, fine_count // fine_step, fine_bulk, 0)
+
     def row_of(ref, n):
         return jnp.broadcast_to(ref[pl.ds(n, 1), :], (ROWS, LANES))
 
-    slot(recv1, me)[...] = slot(send1, me)[...]
-    drain(recv1, r1_sem, peers - 1)
-
     base_code = [((sub + ROWS * g) * 6).astype(jnp.float32) for g in range(coarse_groups)]
     empty = jnp.full((ROWS, LANES), EMPTY, jnp.float32)
+
+    def collect(p, held):
+        held = list(held)
+        for c in range(CAP):
+            key = row_of(recv1, p * ROWS + 2 * CAP + c)
+            values = [row_of(recv1, p * ROWS + 2 * c + which) for which in range(2)]
+            for g in range(coarse_groups):
+                code = key - base_code[g]
+                held[g] = tuple(
+                    jnp.where(code == float(2 * (n // 4) + n % 2), values[n // 2 % 2], held[g][n])
+                    for n in range(12)
+                )
+        return tuple(held)
+
+    slot(recv1, me)[...] = slot(send1, me)[...]
+    drain(recv1, r1_sem.at[0], peers - 2)
+    held = collect(me, ((empty,) * 12,) * coarse_groups)
+    held = each_step(1, peers - 1, lambda k, held: collect(source(k), held), held)
     for g in range(coarse_groups):
-
-        def collect(p, held, g=g):
-            for c in range(CAP):
-                code = row_of(recv1, p * ROWS + 2 * CAP + c) - base_code[g]
-                values = [row_of(recv1, p * ROWS + 2 * c + which) for which in range(2)]
-                held = [
-                    jnp.where(code == float(2 * (n // 4) + n % 2), values[n // 2 % 2], held[n])
-                    for n in range(12)
-                ]
-            return held
-
-        held = lax.fori_loop(0, peers, collect, [empty] * 12, unroll=few)
         for n in range(12):
-            held_ref[plane_slot(n, g), :] = held[n]
-
+            held_ref[plane_slot(n, g), :] = held[g][n]
+    drain(gmax_in, rg_sem, groups - 1)
+    for k in range(1, groups):
+        best = jnp.maximum(best, slot(gmax_in, lax.rem(mg + k, groups))[...])
+    top = jnp.max(jnp.max(best, axis=0, keepdims=True), axis=1, keepdims=True)
+    top_rows[...] = jnp.broadcast_to(top, (ROWS, LANES))
+    drain(recv1, r1_sem.at[1], 1)
+    held = tuple(
+        tuple(held_ref[plane_slot(n, g), :] for n in range(12)) for g in range(coarse_groups)
+    )
+    held = collect(source(jnp.int32(peers - 1)), held)
     spread = row16
     squeeze = EDGE * k8
-
-    def ahead_i(pair):
-        turned = [roll(v, -1) for v in pair]
-        wrapped = [roll(v, HALF - 1) for v in pair]
-        return tuple(jnp.where(k8 == HALF - 1, wrapped[1 - q], turned[q]) for q in range(2))
-
-    def ahead_j(pair):
-        return tuple(
-            jnp.where(
-                last_y,
-                jnp.where(k_of < HALF, roll(v, LANES - EDGE - HALF), roll(v, LANES - HALF)),
-                roll(v, -EDGE),
-            )
-            for v in pair
-        )
+    upper8 = k_of >= HALF
+
+    def known(v):
+        return v < BIG
+
+    def chosen(v, other):
+        return jnp.where(known(v), v, other)
 
     for g in range(coarse_groups):
-        hold = [held_ref[plane_slot(n, g), :] for n in range(12)]
-        sent = [[(hold[4 * d + 2 * w], hold[4 * d + 2 * w + 1]) for w in range(2)] for d in range(3)]
-        now = [
+        for n in range(12):
+            held_ref[plane_slot(n, g), :] = held[g][n]
+        sent = [[[held[g][4 * d + 2 * w + q] for q in range(2)] for w in range(2)] for d in range(3)]
+        base = [
             [
-                [
-                    jnp.where(
-                        sent[d][w][q] < BIG, sent[d][w][q], plane_e[plane_slot(4 * d + 2 * w + q, g), :]
-                    )
-                    for q in range(2)
-                ]
+                [chosen(sent[d][w][q], plane_e[plane_slot(4 * d + 2 * w + q, g), :]) for q in range(2)]
                 for w in range(2)
             ]
             for d in range(3)
         ]
+        now = [[list(base[d][w]) for w in range(2)] for d in range(3)]
+        ahead = [[[None] * 2 for w in range(2)] for d in range(3)]
         for q in range(2):
+            over = roll(sent[2][1][0], -HALF * q)
+            now[0][0][q] = jnp.where(first_z, chosen(over, base[0][0][q]), base[0][0][q])
+            wrap = chosen(roll(sent[2][1][0], EDGE - 1 - HALF * q), roll(base[0][0][q], EDGE - 1))
+            ahead[0][0][q] = jnp.where(last_z, wrap, roll(base[0][0][q], -1))
+
             over = take(sent[2][0][q], spread)
-            now[1][0][q] = jnp.where((over < BIG) & first_z, over, now[1][0][q])
+            now[1][0][q] = jnp.where(first_z, chosen(over, base[1][0][q]), base[1][0][q])
+            wrap = chosen(over, roll(base[1][0][q], EDGE - 1))
+            ahead[1][0][q] = jnp.where(last_z, wrap, roll(base[1][0][q], -1))
+
             under = take(sent[1][0][q], squeeze)
-            free = (sent[2][0][q] >= BIG) & (lane < HALF) & (under < BIG)
-            now[2][0][q] = jnp.where(free, under, now[2][0][q])
-            over = roll(sent[2][1][0], -HALF * q)
-            now[0][0][q] = jnp.where((over < BIG) & first_z, over, now[0][0][q])
-            under = roll(sent[0][0][q], HALF * q)
-            free = (sent[2][1][0] >= BIG) & (k_of == HALF * q) & (under < BIG)
-            now[2][1][0] = jnp.where(free, under, now[2][1][0])
+            free = known(under) & (sent[2][0][q] >= BIG) & (lane < HALF)
+            now[2][0][q] = jnp.where(free, under, base[2][0][q])
+            free = known(under) & (roll(sent[2][0][q], LANES - HALF) >= BIG)
+            wrap = jnp.where(free, under, roll(base[2][0][q], LANES - HALF))
+            wrap = jnp.where(upper8, wrap, roll(base[2][0][q], LANES - EDGE - HALF))
+            ahead[2][0][q] = jnp.where(last_y, wrap, roll(base[2][0][q], -EDGE))
+
         over, under = sent[1][1][0], sent[0][1][0]
-        now[0][1][0] = jnp.where((over < BIG) & first_y, over, now[0][1][0])
-        now[1][1][0] = jnp.where((over >= BIG) & first_y & (under < BIG), under, now[1][1][0])
+        now[0][1][0] = jnp.where(first_y, chosen(over, base[0][1][0]), base[0][1][0])
+        free = known(under) & (over >= BIG) & first_y
+        now[1][1][0] = jnp.where(free, under, base[1][1][0])
+        over, under = roll(over, -EDGE), roll(under, -EDGE)
+        turned = [[roll(base[d][1][q], -EDGE) for q in range(2)] for d in range(2)]
+        wrap = (chosen(over, turned[0][0]), jnp.where(known(under) & (over >= BIG), under, turned[1][0]))
+        for d in range(2):
+            ahead[d][1] = [
+                jnp.where(last_y, turned[d][1], turned[d][0]),
+                jnp.where(last_y, wrap[d], turned[d][1]),
+            ]
+
+        under = jnp.where(upper8, roll(sent[0][0][1], HALF), sent[0][0][0])
+        free = known(under) & (sent[2][1][0] >= BIG) & (k8 == 0)
+        now[2][1][0] = jnp.where(free, under, base[2][1][0])
+        under = jnp.where(upper8, roll(sent[0][0][1], EDGE - 1), roll(sent[0][0][0], HALF - 1))
+        free = known(under) & (roll(sent[2][1][0], HALF - 1) >= BIG)
+        turned = [roll(base[2][1][q], HALF - 1) for q in range(2)]
+        wrap = (turned[1], jnp.where(free, under, turned[0]))
+        for q in range(2):
+            ahead[2][1][q] = jnp.where(k8 == HALF - 1, wrap[q], roll(base[2][1][q], -1))
+
         for d in range(3):
-            one, two = now[d]
-            if d < 2:
-                ahead_one, ahead_two = ahead_y(two), ahead_z(one)
-            else:
-                ahead_one, ahead_two = ahead_i(two), ahead_j(one)
-            left, right = sub2(ahead_one, two), sub2(ahead_two, one)
+            left, right = sub2(ahead[d][1], now[d][1]), sub2(ahead[d][0], now[d][0])
             curl = sub2(right, left) if d == 1 else sub2(left, right)
             for q in range(2):
                 plane_n[plane_slot(2 * d + q, g), :] = curl[q]
 
-    drain(gmax_in, rg_sem, groups - 1)
-    for k in range(1, groups):
-        best = jnp.maximum(best, slot(gmax_in, lax.rem(mg + k, groups))[...])
-    top_row = jnp.broadcast_to(jnp.max(best, axis=0, keepdims=True), (ROWS, LANES))
-
-    def answer(p, carry):
-        rows = top_row
+
+    def answer(p):
+        rows = top_rows[...]
         for c in range(CAP):
             key = row_of(recv1, p * ROWS + 2 * CAP + c)
             curl_acc, field_acc = zero, zero
@@ -549,11 +590,14 @@
             rows = jnp.where(sub == c, sum_rows(curl_acc), rows)
             rows = jnp.where(sub == CAP + c, sum_rows(field_acc), rows)
         slot(send2, p)[...] = rows
+
+    def reply(k, carry):
+        answer(target(k))
+        out2(target(k)).start()
         return carry
 
-    lax.fori_loop(0, peers, answer, 0, unroll=few)
-    each_peer(lambda p: out2(p).start())
-
+    each_step(1, peers, reply)
+    answer(me)
     for g in range(coarse_groups):
         for d in range(3):
             for which in range(2):
@@ -614,16 +658,6 @@
 
     each_pair(pair_normal)
 
-    slot(recv2, me)[...] = slot(send2, me)[...]
-    drain(recv2, r2_sem, peers - 1)
-    top = lax.fori_loop(
-        0, peers, lambda p, t: jnp.maximum(t, row_of(recv2, p * ROWS + 2 * CAP)), zero, unroll=few
-    )
-    step_out[...] = jnp.broadcast_to(0.125 * (0.2 / jnp.max(top, axis=1, keepdims=True)), (ROWS, LANES))
-    for r in range(pair_count):
-        row = owner_of[r] * ROWS + rank_of[r]
-        own_a[r : r + 1, :] = recv2[pl.ds(row, 1), :]
-        own_b[r : r + 1, :] = recv2[pl.ds(row + CAP, 1), :]
     for s in range(0, pair_count, ROWS):
         turned, column_of = jnp.zeros_like(lane), jnp.zeros_like(lane)
         for r in range(s, min(s + ROWS, pair_count)):
@@ -631,34 +665,54 @@
             column_of = jnp.where(sub == r - s, pairs[r, 5], column_of)
         for h in range(2):
             m, n = 4 * h + lane // 32, k_of // 2
-            index = jnp.where(turned == 2, EDGE * n + m, EDGE * m + n) + HALF * column_of
-            curl, field = take(own_a[s : s + ROWS, :], index), take(own_b[s : s + ROWS, :], index)
-            side = slice(h * LANES, (h + 1) * LANES)
-            fine = [picked[n * pair_rows + s : n * pair_rows + s + ROWS, :] for n in (h, 2 + h)]
-            jump_a[s : s + ROWS, side] = fine[0] - field
-            jump_b[s : s + ROWS, side] = 2.0 * fine[1] - curl
+            index_out[h * pair_rows + s : h * pair_rows + s + ROWS, :] = (
+                jnp.where(turned == 2, EDGE * n + m, EDGE * m + n) + HALF * column_of
+            )
+
+    slot(recv2, me)[...] = slot(send2, me)[...]
+    drain(recv2, r2_sem, peers - 1)
+    for r in range(pair_count):
+        row = owner_of[r] * ROWS + rank_of[r]
+        own_a[r : r + 1, :] = recv2[pl.ds(row, 1), :]
+        own_b[r : r + 1, :] = recv2[pl.ds(row + CAP, 1), :]
+    top = lax.fori_loop(
+        0, peers, lambda p, t: jnp.maximum(t, row_of(recv2, p * ROWS + 2 * CAP)), zero, unroll=few
+    )
+    step_out[...] = 0.125 * (0.2 / top)
     drain(send1, s1_sem, peers - 1)
     drain(send2, s2_sem, peers - 1)
     drain(gmax_in, sg_sem, groups - 1)
 
 
-def store(cb, curl_c, fb, curl_f, jump_a, jump_b, step, out_c, out_f, out_j, new_c, new_f, new_j, sems):
+def store(
+    cb, curl_c, fb, curl_f, picked, own_a, own_b, index, step, out_c, out_f, out_j, new_c, new_f, new_j, sems
+):
     by = step[0:1, 0:1]
     copies = []
+
+    def send(src, dst):
+        copies.append(pltpu.make_async_copy(src, dst, sems.at[len(copies)]))
+        copies[-1].start()
+
     for c in range(3):
         new_c[c] = cb[c] - by * curl_c[c]
-        copies.append(pltpu.make_async_copy(new_c.at[c], out_c.at[c], sems.at[len(copies)]))
-        copies[-1].start()
+        send(new_c.at[c], out_c.at[c])
     rows = fb.shape[0]
     for n in range(2):
         part = pl.ds(n * (rows // 2), rows // 2)
         new_f[part, :] = fb[part, :] - (2.0 * by) * curl_f[part, :]
-        copies.append(pltpu.make_async_copy(new_f.at[part], out_f.at[part], sems.at[len(copies)]))
-        copies[-1].start()
-    count = out_j.shape[0]
-    new_j[...] = (jump_a[...] - by * jump_b[...])[:count]
-    copies.append(pltpu.make_async_copy(new_j, out_j, sems.at[len(copies)]))
-    copies[-1].start()
+        send(new_f.at[part], out_f.at[part])
+    count, pair_rows = out_j.shape[0], own_a.shape[0]
+    for s in range(0, count, ROWS):
+        for h in range(2):
+            fine, curl, column = [
+                ref[n * pair_rows + s : n * pair_rows + s + ROWS, :]
+                for ref, n in ((picked, h), (picked, 2 + h), (index, h))
+            ]
+            fine = fine - (2.0 * by) * curl
+            coarse = own_b[s : s + ROWS, :] - by * own_a[s : s + ROWS, :]
+            new_j[s : s + ROWS, h * LANES : (h + 1) * LANES] = fine - take(coarse, column)
+    send(new_j.at[pl.ds(0, count)], out_j)
     for copy in copies:
         copy.wait()
 
@@ -697,13 +751,16 @@
         coarse_shape,
         fine_shape,
         fine_shape,
-        (pair_rows, EDGE * EDGE),
-        (pair_rows, EDGE * EDGE),
+        (4 * pair_rows, LANES),
+        (pair_rows, LANES),
+        (pair_rows, LANES),
+        (2 * pair_rows, LANES),
         (ROWS, LANES),
     )
+    kinds = [f32] * 7 + [jnp.int32, f32]
     results = pl.pallas_call(
         functools.partial(kernel, peers, groups, coarse_count, fine_count, pair_count),
-        out_shape=tuple(jax.ShapeDtypeStruct(s, f32) for s in shapes),
+        out_shape=tuple(jax.ShapeDtypeStruct(s, k) for s, k in zip(shapes, kinds)),
         in_specs=[anywhere] * 5,
         out_specs=(inside,) * len(shapes),
         scratch_shapes=[
@@ -712,15 +769,13 @@
             vmem(fine_shape, f32),
             vmem(coarse_shape, f32),
             vmem((pair_count * SPAN, LANES), f32),
-            vmem((6 * CHUNK * coarse_count, LANES), f32),
-            vmem((2 * CHUNK * coarse_count, LANES), f32),
+            vmem((6 * EDGE * coarse_count, LANES), f32),
+            vmem((2 * EDGE * coarse_count, LANES), f32),
             vmem((12 * coarse_count, LANES), f32),
             vmem((6 * coarse_count, LANES), f32),
             vmem((6 * coarse_count, LANES), f32),
             vmem((12 * coarse_count, LANES), f32),
-            vmem((pair_rows, LANES), f32),
-            vmem((pair_rows, LANES), f32),
-            vmem((4 * pair_rows, LANES), f32),
+            vmem((ROWS, LANES), f32),
             vmem((4 * pair_rows, LANES), f32),
             vmem((peers * ROWS, LANES), f32),
             vmem((peers * ROWS, LANES), f32),
@@ -730,7 +785,7 @@
             vmem((groups * ROWS, LANES), f32),
             dma((5,)),
             dma,
-            dma,
+            dma((2,)),
             dma,
             dma,
             dma,
@@ -752,7 +807,7 @@
         scratch_shapes=[
             vmem(coarse_shape, f32),
             vmem(fine_shape, f32),
-            vmem((pair_count, EDGE * EDGE), f32),
+            vmem((pair_rows, EDGE * EDGE), f32),
             dma((6,)),
         ],
     )(*(pltpu.with_memory_space_constraint(x, pltpu.VMEM) for x in results))

time: 16.7 us -> 16.2 us (0.970)
  Pallas kernels: 15.9 us -> 15.4 us
    pallas_call x1, Pallas kernels: 14.7 us -> 14.2 us  [on_device(): pl.pallas_call(functools.partial(kernel, peers, groups, coarse_count, fin...]
where the time goes in v3:
time: 16.2 us; the launch traced here: 16.1 us
  Pallas kernels  15.4 us (95%)
  between operations  0.64 us (4%)
    pallas_call x1, Pallas kernels, on_device(): pl.pallas_call(functools.partial(kernel, peers, groups, coarse_count, fin...  14.2 us
    pallas_call x1, Pallas kernels, on_device(): pl.pallas_call(store, out_shape=(jax.ShapeDtypeStruct(coarse_shape, f32),...  1.2 us

profile of v3, /device:TPU:0, one launch (start us, length us, event | category | flops | bytes accessed | tf_op | source)
XLA Modules:
  0.0 16.1 jit_solution(11694644645119469171)
XLA Ops:
  0.6 14.2 %shard_map.76 = (f32[3,16,4096]{2,1,0:T(8,128)S(1)}, f32[3,16,4096]{2,1,0:T(8,128)S(1)}, f32[1152,128]{1,0:T(8,128)S(1)}, f32[1152,128]{1,0:T(8,128)S(1)}, f32[3...) custom-call(s32[4,6]{1,0:T(4,128)} %bitcast.18, ...), custom_call_target="tpu_custom_call" | custom-call | tf_op jit(solution)/shard_map/pallas_call | solution.py:761
  14.9 1.2 %shard_map.77 = (f32[3,16,4096]{2,1,0:T(8,128)}, f32[1152,128]{1,0:T(8,128)}, f32[4,256]{1,0:T(4,128)}) custom-call(f32[3,16,4096]{2,1,0:T(8,128)S(1)} %get-tuple-element.15.cb, f32[3,16,4096]{2,1,0:T(8,128)S(1)} %get-tuple-element.16.curl_c, f32[1152,128]{1,0:T(8,128)S(1)} %get-tuple-element.17.fb, f32[1152,128]{1,0:T(8,128)S(1)} %get-tuple-element.18.curl_f, ...), custom_call_target="tpu_custom_call" | custom-call | tf_op jit(solution)/shard_map/pallas_call | solution.py:798

commit v4 on v3

--- a/solution.py
+++ b/solution.py
@@ -45,17 +45,17 @@
     cv_hbm,
     fb_hbm,
     fv_hbm,
-    cb,
     curl_c,
-    fb,
     curl_f,
-    picked,
+    fine_face,
     own_a,
     own_b,
     index_out,
     step_out,
     pairs,
+    cb,
     cv,
+    fb,
     fv,
     emf_c,
     emf_p,
@@ -65,7 +65,8 @@
     plane_b,
     plane_n,
     held_ref,
-    top_rows,
+    picked,
+    tops,
     rows1,
     send1,
     recv1,
@@ -74,12 +75,11 @@
     gmax,
     gmax_in,
     load_sem,
-    s1_sem,
+    sent_sem,
     r1_sem,
-    s2_sem,
     r2_sem,
-    sg_sem,
     rg_sem,
+    rt_sem,
 ):
     me = lax.axis_index("blocks")
     mg = lax.axis_index("gz")
@@ -88,24 +88,25 @@
     pair_rows = ROWS * -(-pair_count // ROWS)
 
     paired = peers & (peers - 1) == 0
-    bits = [1 << n for n in range(peers.bit_length() - 1)]
+    flips = []
+    for n in range(peers.bit_length() - 1):
+        bit = 1 << n
+        flips.append((bit, bit * (1 - 2 * lax.rem(lax.div(me, bit), 2))))
 
     def target(k):
         if not paired:
             return lax.rem(me + k, peers)
-        p = me
-        for bit in bits:
-            p = p + lax.rem(k // bit, 2) * bit * (1 - 2 * lax.rem(me // bit, 2))
-        return p
+        return sum((lax.rem(lax.div(k, bit), 2) * flip for bit, flip in flips), me)
 
     def source(k):
         return target(k) if paired else lax.rem(me + peers - k, peers)
 
     def each_step(first, last, body, carry=0):
-        def step(n, carry):
-            return body(last - 1 - n, carry)
-
-        return lax.fori_loop(0, last - first, step, carry, unroll=few)
+        if few:
+            for k in range(last - 1, first - 1, -1):
+                carry = body(k, carry)
+            return carry
+        return lax.fori_loop(0, last - first, lambda n, c: body(last - 1 - n, c), carry)
 
     def each_peer(body):
         each_step(1, peers, lambda k, _: (body(target(k)), 0)[1])
@@ -373,35 +374,45 @@
         return functools.reduce(jnp.maximum, tops, best)
 
     best = lax.fori_loop(0, EDGE // TOP_CHUNK, coarse_top, best)
-    gmax[...] = best
+    gmax[...] = jnp.max(best, axis=0, keepdims=True)
 
     pl.semaphore_wait(barrier, peers - 1 + groups - 1)
+
+    def part(ref, p, rows):
+        return ref.at[pl.ds(pl.multiple_of(p * ROWS, ROWS), rows)]
 
     def out1(k):
         p = target(k)
         return pltpu.make_async_remote_copy(
-            src_ref=slot(send1, p), dst_ref=slot(recv1, me), send_sem=s1_sem,
+            src_ref=part(send1, p, 3 * CAP), dst_ref=part(recv1, me, 3 * CAP), send_sem=sent_sem,
             recv_sem=r1_sem.at[k // (peers - 1)], device_id=(p, mg), device_id_type=MESH,
         )
 
     def out2(p):
         return pltpu.make_async_remote_copy(
-            src_ref=slot(send2, p), dst_ref=slot(recv2, me), send_sem=s2_sem,
+            src_ref=part(send2, p, 2 * CAP), dst_ref=part(recv2, me, 2 * CAP), send_sem=sent_sem,
             recv_sem=r2_sem, device_id=(p, mg), device_id_type=MESH,
         )
 
     def outg(g):
         return pltpu.make_async_remote_copy(
-            src_ref=gmax, dst_ref=slot(gmax_in, mg), send_sem=sg_sem,
+            src_ref=gmax, dst_ref=gmax_in.at[pl.ds(mg, 1)], send_sem=sent_sem,
             recv_sem=rg_sem, device_id=(me, g), device_id_type=MESH,
         )
 
-    def drain(ref, sem, count):
-        part = ref.at[pl.ds(0, ROWS * count)]
-        pltpu.make_async_copy(part, part, sem).wait()
-
+    def outt(p):
+        return pltpu.make_async_remote_copy(
+            src_ref=tops.at[pl.ds(me, 1)], dst_ref=tops.at[pl.ds(me, 1)], send_sem=sent_sem,
+            recv_sem=rt_sem, device_id=(p, mg), device_id_type=MESH,
+        )
+
+    def drain(ref, sem, rows):
+        whole = ref.at[pl.ds(0, rows)]
+        pltpu.make_async_copy(whole, whole, sem).wait()
+
+    out1(peers - 1).start()
     each_group(lambda g: outg(g).start())
-    each_step(1, peers, lambda k, _: (out1(k).start(), 0)[1])
+    each_step(1, peers - 1, lambda k, _: (out1(k).start(), 0)[1])
 
 
     def coarse_step(t, parts):
@@ -488,18 +499,19 @@
         return tuple(held)
 
     slot(recv1, me)[...] = slot(send1, me)[...]
-    drain(recv1, r1_sem.at[0], peers - 2)
+    drain(recv1, r1_sem.at[0], (peers - 2) * 3 * CAP)
     held = collect(me, ((empty,) * 12,) * coarse_groups)
     held = each_step(1, peers - 1, lambda k, held: collect(source(k), held), held)
     for g in range(coarse_groups):
         for n in range(12):
             held_ref[plane_slot(n, g), :] = held[g][n]
     drain(gmax_in, rg_sem, groups - 1)
+    best = gmax[...]
     for k in range(1, groups):
-        best = jnp.maximum(best, slot(gmax_in, lax.rem(mg + k, groups))[...])
-    top = jnp.max(jnp.max(best, axis=0, keepdims=True), axis=1, keepdims=True)
-    top_rows[...] = jnp.broadcast_to(top, (ROWS, LANES))
-    drain(recv1, r1_sem.at[1], 1)
+        best = jnp.maximum(best, gmax_in[pl.ds(lax.rem(mg + k, groups), 1), :])
+    tops[pl.ds(me, 1), :] = jnp.broadcast_to(jnp.max(best, axis=1, keepdims=True), (1, LANES))
+    each_peer(lambda p: outt(p).start())
+    drain(recv1, r1_sem.at[1], 3 * CAP)
     held = tuple(
         tuple(held_ref[plane_slot(n, g), :] for n in range(12)) for g in range(coarse_groups)
     )
@@ -577,7 +589,7 @@
 
 
     def answer(p):
-        rows = top_rows[...]
+        rows = zero
         for c in range(CAP):
             key = row_of(recv1, p * ROWS + 2 * CAP + c)
             curl_acc, field_acc = zero, zero
@@ -669,50 +681,59 @@
                 jnp.where(turned == 2, EDGE * n + m, EDGE * m + n) + HALF * column_of
             )
 
+    drain(tops, rt_sem, peers - 1)
+    by = jnp.broadcast_to(
+        0.125 * (0.2 / jnp.max(tops[...], axis=0, keepdims=True)), (ROWS, LANES)
+    )
+    step_out[...] = by
+
+    def finish_coarse(i, carry):
+        for g in range(coarse_groups):
+            field, curl, put = blocked(cb, g), blocked(curl_c, g), blocked_put(curl_c, g)
+            for c in range(3):
+                put(c, i, sub2(field(c, i), mul((by, by), curl(c, i))))
+        return carry
+
+    lax.fori_loop(0, EDGE, finish_coarse, 0, unroll=4)
+    twice = 2.0 * by
+    tiles = largest_step(fine_count * SPAN // ROWS, 36)
+
+    def finish_fine(n, carry):
+        for u in range(tiles):
+            rows = pl.ds(pl.multiple_of((n * tiles + u) * ROWS, ROWS), ROWS)
+            curl_f[rows, :] = fb[rows, :] - twice * curl_f[rows, :]
+        return carry
+
+    lax.fori_loop(0, fine_count * SPAN // ROWS // tiles, finish_fine, 0)
+    for n in range(0, 2 * pair_rows, ROWS):
+        far = slice(2 * pair_rows + n, 2 * pair_rows + n + ROWS)
+        fine_face[n : n + ROWS, :] = picked[n : n + ROWS, :] - twice * picked[far, :]
     slot(recv2, me)[...] = slot(send2, me)[...]
-    drain(recv2, r2_sem, peers - 1)
+    drain(recv2, r2_sem, (peers - 1) * 2 * CAP)
     for r in range(pair_count):
         row = owner_of[r] * ROWS + rank_of[r]
         own_a[r : r + 1, :] = recv2[pl.ds(row, 1), :]
         own_b[r : r + 1, :] = recv2[pl.ds(row + CAP, 1), :]
-    top = lax.fori_loop(
-        0, peers, lambda p, t: jnp.maximum(t, row_of(recv2, p * ROWS + 2 * CAP)), zero, unroll=few
-    )
-    step_out[...] = 0.125 * (0.2 / top)
-    drain(send1, s1_sem, peers - 1)
-    drain(send2, s2_sem, peers - 1)
-    drain(gmax_in, sg_sem, groups - 1)
-
-
-def store(
-    cb, curl_c, fb, curl_f, picked, own_a, own_b, index, step, out_c, out_f, out_j, new_c, new_f, new_j, sems
-):
-    by = step[0:1, 0:1]
-    copies = []
-
-    def send(src, dst):
-        copies.append(pltpu.make_async_copy(src, dst, sems.at[len(copies)]))
-        copies[-1].start()
-
-    for c in range(3):
-        new_c[c] = cb[c] - by * curl_c[c]
-        send(new_c.at[c], out_c.at[c])
-    rows = fb.shape[0]
-    for n in range(2):
-        part = pl.ds(n * (rows // 2), rows // 2)
-        new_f[part, :] = fb[part, :] - (2.0 * by) * curl_f[part, :]
-        send(new_f.at[part], out_f.at[part])
+    drain(fb, sent_sem, (peers - 1) * (5 * CAP + 1) + groups - 1)
+
+
+def store(new_c, new_f, fine_face, own_a, own_b, index, step, out_c, out_f, out_j, new_j, sems):
+    copies = [
+        pltpu.make_async_copy(src, dst, sems.at[n])
+        for n, (src, dst) in enumerate(((new_c, out_c), (new_f, out_f)))
+    ]
+    for copy in copies:
+        copy.start()
     count, pair_rows = out_j.shape[0], own_a.shape[0]
     for s in range(0, count, ROWS):
+        coarse = own_b[s : s + ROWS, :] - step[...] * own_a[s : s + ROWS, :]
         for h in range(2):
-            fine, curl, column = [
-                ref[n * pair_rows + s : n * pair_rows + s + ROWS, :]
-                for ref, n in ((picked, h), (picked, 2 + h), (index, h))
-            ]
-            fine = fine - (2.0 * by) * curl
-            coarse = own_b[s : s + ROWS, :] - by * own_a[s : s + ROWS, :]
-            new_j[s : s + ROWS, h * LANES : (h + 1) * LANES] = fine - take(coarse, column)
-    send(new_j.at[pl.ds(0, count)], out_j)
+            here = slice(h * pair_rows + s, h * pair_rows + s + ROWS)
+            new_j[s : s + ROWS, h * LANES : (h + 1) * LANES] = fine_face[here, :] - take(
+                coarse, index[here, :]
+            )
+    copies.append(pltpu.make_async_copy(new_j.at[pl.ds(0, count)], out_j, sems.at[2]))
+    copies[-1].start()
     for copy in copies:
         copy.wait()
 
@@ -748,16 +769,14 @@
     coarse_shape, fine_shape = (3, coarse_count, cells), (flat_rows, LANES)
     shapes = (
         coarse_shape,
-        coarse_shape,
         fine_shape,
-        fine_shape,
-        (4 * pair_rows, LANES),
+        (2 * pair_rows, LANES),
         (pair_rows, LANES),
         (pair_rows, LANES),
         (2 * pair_rows, LANES),
         (ROWS, LANES),
     )
-    kinds = [f32] * 7 + [jnp.int32, f32]
+    kinds = [f32] * 5 + [jnp.int32, f32]
     results = pl.pallas_call(
         functools.partial(kernel, peers, groups, coarse_count, fine_count, pair_count),
         out_shape=tuple(jax.ShapeDtypeStruct(s, k) for s, k in zip(shapes, kinds)),
@@ -766,6 +785,8 @@
         scratch_shapes=[
             pltpu.SMEM(pairs.shape[1:], jnp.int32),
             vmem(coarse_shape, f32),
+            vmem(coarse_shape, f32),
+            vmem(fine_shape, f32),
             vmem(fine_shape, f32),
             vmem(coarse_shape, f32),
             vmem((pair_count * SPAN, LANES), f32),
@@ -775,18 +796,18 @@
             vmem((6 * coarse_count, LANES), f32),
             vmem((6 * coarse_count, LANES), f32),
             vmem((12 * coarse_count, LANES), f32),
-            vmem((ROWS, LANES), f32),
+            vmem((4 * pair_rows, LANES), f32),
+            vmem((peers, LANES), f32),
             vmem((4 * pair_rows, LANES), f32),
             vmem((peers * ROWS, LANES), f32),
             vmem((peers * ROWS, LANES), f32),
             vmem((peers * ROWS, LANES), f32),
             vmem((peers * ROWS, LANES), f32),
-            vmem((ROWS, LANES), f32),
-            vmem((groups * ROWS, LANES), f32),
+            vmem((1, LANES), f32),
+            vmem((groups, LANES), f32),
             dma((5,)),
             dma,
             dma((2,)),
-            dma,
             dma,
             dma,
             dma,
@@ -805,10 +826,8 @@
         in_specs=[inside] * len(shapes),
         out_specs=(anywhere,) * 3,
         scratch_shapes=[
-            vmem(coarse_shape, f32),
-            vmem(fine_shape, f32),
             vmem((pair_rows, EDGE * EDGE), f32),
-            dma((6,)),
+            dma((3,)),
         ],
     )(*(pltpu.with_memory_space_constraint(x, pltpu.VMEM) for x in results))
     return (

time: 16.2 us -> 16.1 us (level)
  no operation moved by 1% of the time
where the time goes in v4:
time: 16.1 us; the launch traced here: 15.9 us
  Pallas kernels  15.3 us (95%)
  between operations  0.64 us (4%)
    pallas_call x1, Pallas kernels, on_device(): pl.pallas_call(functools.partial(kernel, peers, groups, coarse_count, fin...  14.2 us
    pallas_call x1, Pallas kernels, on_device(): pl.pallas_call(store, out_shape=(jax.ShapeDtypeStruct(coarse_shape, f32),...  1.11 us

profile of v4, /device:TPU:0, one launch (start us, length us, event | category | flops | bytes accessed | tf_op | source)
XLA Modules:
  0.0 15.9 jit_solution(17482806981180071932)
XLA Ops:
  0.6 14.2 %shard_map.76 = (f32[3,16,4096]{2,1,0:T(8,128)S(1)}, f32[1152,128]{1,0:T(8,128)S(1)}, f32[16,128]{1,0:T(8,128)S(1)}, f32[8,128]{1,0:T(8,128)S(1)}, f32[8,128]{1,...) custom-call(s32[4,6]{1,0:T(4,128)} %bitcast.18, f32[3,16,4096]{2,1,0:T(8,128)} %bitcast.14, ...), custom_call_target="tpu_custom_call" | custom-call | tf_op jit(solution)/shard_map/pallas_call | solution.py:780
  14.8 1.1 %shard_map.77 = (f32[3,16,4096]{2,1,0:T(8,128)}, f32[1152,128]{1,0:T(8,128)}, f32[4,256]{1,0:T(4,128)}) custom-call(f32[3,16,4096]{2,1,0:T(8,128)S(1)} %get-tuple-element.13.new_c, f32[1152,128]{1,0:T(8,128)S(1)} %get-tuple-element.14.new_f, f32[16,128]{1,0:T(8,128)S(1)} %get-tuple-element.15.fine_face, f32[8,128]{1,0:T(8,128)S(1)} %get-tuple-element.16.own_a, ...), custom_call_target="tpu_custom_call" | custom-call | tf_op jit(solution)/shard_map/pallas_call | solution.py:819

commit v5 on v4

--- a/solution.py
+++ b/solution.py
@@ -70,12 +70,16 @@
     rows1,
     send1,
     recv1,
+    relayed,
     send2,
     recv2,
     gmax,
     gmax_in,
     load_sem,
     sent_sem,
+    s1_sem,
+    bundle_sem,
+    go_sem,
     r1_sem,
     r2_sem,
     rg_sem,
@@ -116,9 +120,15 @@
             body(lax.rem(mg + k, groups))
 
     barrier = pltpu.get_barrier_semaphore()
-    each_peer(
-        lambda p: pl.semaphore_signal(barrier, inc=1, device_id=(p, mg), device_id_type=MESH)
-    )
+    relay = paired and few and peers > 2
+    early = peers // 2 if relay else 0
+    greeted = peers - 1 + groups - 1
+
+    def greet(p):
+        at = jnp.where(jnp.logical_and(p == 0, me > 1), 1, p) if relay else p
+        pl.semaphore_signal(barrier, inc=1, device_id=(at, mg), device_id_type=MESH)
+
+    each_peer(greet)
     loads = [
         pltpu.make_async_copy(src, dst, load_sem.at[n])
         for n, (src, dst) in enumerate(((fb_hbm, fb), (fv_hbm, fv), (cb_hbm, cb), (cv_hbm, cv)))
@@ -127,8 +137,9 @@
     listed.start()
     for load in loads:
         load.start()
+    me_or_one = jnp.where(me == 0, 1, me) if relay else me
     each_group(
-        lambda g: pl.semaphore_signal(barrier, inc=1, device_id=(me, g), device_id_type=MESH)
+        lambda g: pl.semaphore_signal(barrier, inc=1, device_id=(me_or_one, g), device_id_type=MESH)
     )
 
     lane = lax.broadcasted_iota(jnp.int32, (ROWS, LANES), 1)
@@ -243,9 +254,132 @@
     def sum_rows(v):
         return jnp.sum(v, axis=0, keepdims=True)
 
-    listed.wait()
+    def column(tile):
+        return pl.ds(pl.multiple_of(tile * LANES, LANES), LANES)
+
+    def blocked(ref, g):
+        def read(c, i):
+            return tuple(ref[c, ROWS * g : ROWS * g + ROWS, column(2 * i + h)] for h in range(2))
+
+        return read
+
+    def blocked_put(ref, g):
+        def put(c, i, pair):
+            for h in range(2):
+                ref[c, ROWS * g : ROWS * g + ROWS, column(2 * i + h)] = pair[h]
+
+        return put
+
     loads[0].wait()
     loads[1].wait()
+
+    speed_step = largest_step(fine_count, SPEED_STEP)
+
+    def fine_top(n, best):
+        for u in range(speed_step):
+            base = (n * speed_step + u) * SPAN
+            b, v = fine_read(fb, base), fine_read(fv, base)
+            best = jnp.maximum(best, top_of(v, fine_centre(b)))
+        return best
+
+    best = lax.fori_loop(0, fine_count // speed_step, fine_top, zero)
+
+    loads[2].wait()
+    loads[3].wait()
+
+
+    def at(n, i, g, h):
+        row = (((n * coarse_groups + g) * EDGE + i) * 2 + h) * ROWS
+        return pl.ds(row if isinstance(row, int) else pl.multiple_of(row, ROWS), ROWS)
+
+    def each_plane(chunk, planes, body):
+        for u in range(planes):
+            for g in range(coarse_groups):
+                body(chunk * planes + u, g)
+
+    def coarse_top(n, best):
+        tops = []
+
+        def plane(i, g):
+            field = blocked(cb, g)
+            b = [field(c, i) for c in range(3)]
+            c = (
+                add(b[0], field(0, lax.rem(i + 1, EDGE))),
+                add(b[1], ahead_y(b[1])),
+                add(b[2], ahead_z(b[2])),
+            )
+            for k in range(3):
+                for h in range(2):
+                    centred[at(k, i, g, h), :] = c[k][h]
+            tops.append(top_of([blocked(cv, g)(k, i) for k in range(3)], c))
+
+        each_plane(n, TOP_CHUNK, plane)
+        return functools.reduce(jnp.maximum, tops, best)
+
+    best = lax.fori_loop(0, EDGE // TOP_CHUNK, coarse_top, best)
+    gmax[...] = jnp.max(best, axis=0, keepdims=True)
+
+    def slot(ref, p):
+        return ref.at[pl.ds(pl.multiple_of(p * ROWS, ROWS), ROWS)]
+
+    def part(ref, p, rows):
+        return ref.at[pl.ds(pl.multiple_of(p * ROWS, ROWS), rows)]
+
+    def out1(k):
+        p = target(k)
+        return pltpu.make_async_remote_copy(
+            src_ref=part(send1, p, 3 * CAP), dst_ref=part(recv1, me, 3 * CAP), send_sem=s1_sem,
+            recv_sem=r1_sem.at[k // (peers - 1)], device_id=(p, mg), device_id_type=MESH,
+        )
+
+    def out2(p):
+        return pltpu.make_async_remote_copy(
+            src_ref=part(send2, p, 2 * CAP), dst_ref=part(recv2, me, 2 * CAP), send_sem=sent_sem,
+            recv_sem=r2_sem, device_id=(p, mg), device_id_type=MESH,
+        )
+
+    def outg(g):
+        return pltpu.make_async_remote_copy(
+            src_ref=gmax, dst_ref=gmax_in.at[pl.ds(mg, 1)], send_sem=sent_sem,
+            recv_sem=rg_sem, device_id=(me, g), device_id_type=MESH,
+        )
+
+    def outt(p):
+        return pltpu.make_async_remote_copy(
+            src_ref=tops.at[pl.ds(me, 1)], dst_ref=tops.at[pl.ds(me, 1)], send_sem=sent_sem,
+            recv_sem=rt_sem, device_id=(p, mg), device_id_type=MESH,
+        )
+
+    def drain(ref, sem, rows):
+        whole = ref.at[pl.ds(0, rows)]
+        pltpu.make_async_copy(whole, whole, sem).wait()
+
+    def out_bundle():
+        rows = pl.ds(2 * ROWS, (peers - 2) * ROWS)
+        return pltpu.make_async_remote_copy(
+            src_ref=send1.at[rows], dst_ref=relayed.at[rows], send_sem=s1_sem,
+            recv_sem=bundle_sem, device_id=(1, mg), device_id_type=MESH,
+        )
+
+    def out_relay(p):
+        return pltpu.make_async_remote_copy(
+            src_ref=part(relayed, p, 3 * CAP), dst_ref=part(recv1, 0, 3 * CAP), send_sem=s1_sem,
+            recv_sem=r1_sem.at[p // (peers - 1)], device_id=(p, mg), device_id_type=MESH,
+        )
+
+    def send_all():
+        each_step(1, peers, lambda k, _: (out1(k).start(), 0)[1])
+
+    def send_group():
+        each_group(lambda g: outg(g).start())
+
+
+    @pl.when(me >= early)
+    def _():
+        pl.semaphore_wait(barrier, greeted)
+        send_group()
+
+    listed.wait()
 
     half_lane = 32 * (row16 % 4)
     index_r = (half_lane + 2 * k8, 2 * k8, half_lane)
@@ -309,110 +443,44 @@
         slot(send1, p)[...] = message
         return carry
 
-    def slot(ref, p):
-        return ref.at[pl.ds(pl.multiple_of(p * ROWS, ROWS), ROWS)]
-
     lax.fori_loop(0, peers, build, 0, unroll=few)
 
-    def column(tile):
-        return pl.ds(pl.multiple_of(tile * LANES, LANES), LANES)
-
-    def blocked(ref, g):
-        def read(c, i):
-            return tuple(ref[c, ROWS * g : ROWS * g + ROWS, column(2 * i + h)] for h in range(2))
-
-        return read
-
-    def blocked_put(ref, g):
-        def put(c, i, pair):
-            for h in range(2):
-                ref[c, ROWS * g : ROWS * g + ROWS, column(2 * i + h)] = pair[h]
-
-        return put
-
-    speed_step = largest_step(fine_count, SPEED_STEP)
-
-    def fine_top(n, best):
-        for u in range(speed_step):
-            base = (n * speed_step + u) * SPAN
-            b, v = fine_read(fb, base), fine_read(fv, base)
-            best = jnp.maximum(best, top_of(v, fine_centre(b)))
-        return best
-
-    best = lax.fori_loop(0, fine_count // speed_step, fine_top, zero)
-
-    loads[2].wait()
-    loads[3].wait()
-
-
-    def at(n, i, g, h):
-        row = (((n * coarse_groups + g) * EDGE + i) * 2 + h) * ROWS
-        return pl.ds(row if isinstance(row, int) else pl.multiple_of(row, ROWS), ROWS)
-
-    def each_plane(chunk, planes, body):
-        for u in range(planes):
-            for g in range(coarse_groups):
-                body(chunk * planes + u, g)
-
-    def coarse_top(n, best):
-        tops = []
-
-        def plane(i, g):
-            field = blocked(cb, g)
-            b = [field(c, i) for c in range(3)]
-            c = (
-                add(b[0], field(0, lax.rem(i + 1, EDGE))),
-                add(b[1], ahead_y(b[1])),
-                add(b[2], ahead_z(b[2])),
-            )
-            for k in range(3):
-                for h in range(2):
-                    centred[at(k, i, g, h), :] = c[k][h]
-            tops.append(top_of([blocked(cv, g)(k, i) for k in range(3)], c))
-
-        each_plane(n, TOP_CHUNK, plane)
-        return functools.reduce(jnp.maximum, tops, best)
-
-    best = lax.fori_loop(0, EDGE // TOP_CHUNK, coarse_top, best)
-    gmax[...] = jnp.max(best, axis=0, keepdims=True)
-
-    pl.semaphore_wait(barrier, peers - 1 + groups - 1)
-
-    def part(ref, p, rows):
-        return ref.at[pl.ds(pl.multiple_of(p * ROWS, ROWS), rows)]
-
-    def out1(k):
-        p = target(k)
-        return pltpu.make_async_remote_copy(
-            src_ref=part(send1, p, 3 * CAP), dst_ref=part(recv1, me, 3 * CAP), send_sem=sent_sem,
-            recv_sem=r1_sem.at[k // (peers - 1)], device_id=(p, mg), device_id_type=MESH,
-        )
-
-    def out2(p):
-        return pltpu.make_async_remote_copy(
-            src_ref=part(send2, p, 2 * CAP), dst_ref=part(recv2, me, 2 * CAP), send_sem=sent_sem,
-            recv_sem=r2_sem, device_id=(p, mg), device_id_type=MESH,
-        )
-
-    def outg(g):
-        return pltpu.make_async_remote_copy(
-            src_ref=gmax, dst_ref=gmax_in.at[pl.ds(mg, 1)], send_sem=sent_sem,
-            recv_sem=rg_sem, device_id=(me, g), device_id_type=MESH,
-        )
-
-    def outt(p):
-        return pltpu.make_async_remote_copy(
-            src_ref=tops.at[pl.ds(me, 1)], dst_ref=tops.at[pl.ds(me, 1)], send_sem=sent_sem,
-            recv_sem=rt_sem, device_id=(p, mg), device_id_type=MESH,
-        )
-
-    def drain(ref, sem, rows):
-        whole = ref.at[pl.ds(0, rows)]
-        pltpu.make_async_copy(whole, whole, sem).wait()
-
-    out1(peers - 1).start()
-    each_group(lambda g: outg(g).start())
-    each_step(1, peers - 1, lambda k, _: (out1(k).start(), 0)[1])
+    if relay:
+
+        @pl.when(me == 0)
+        def _():
+            pl.semaphore_wait(barrier, 1)
+            out1(1).start()
+            out_bundle().start()
+
+        @pl.when(me == 1)
+        def _():
+            pl.semaphore_wait(barrier, greeted + groups - 1 + peers - 2)
+            pl.semaphore_signal(go_sem, inc=1, device_id=(0, mg), device_id_type=MESH)
+            rows = relayed.at[pl.ds(2 * ROWS, (peers - 2) * ROWS)]
+            pltpu.make_async_copy(rows, rows, bundle_sem).wait()
+            for p in range(peers - 1, 1, -1):
+                out_relay(p).start()
+
+        @pl.when(jnp.logical_and(me > 1, me < early))
+        def _():
+            pl.semaphore_wait(barrier, greeted)
+
+        @pl.when(me > 0)
+        def _():
+            send_all()
+
+
+        @pl.when(me == 0)
+        def _():
+            pl.semaphore_wait(go_sem, 1)
+
+        @pl.when(me < early)
+        def _():
+            send_group()
+
+    else:
+        send_all()
 
 
     def coarse_step(t, parts):
@@ -498,6 +566,12 @@
                 )
         return tuple(held)
 
+    drain(gmax_in, rg_sem, groups - 1)
+    best = gmax[...]
+    for k in range(1, groups):
+        best = jnp.maximum(best, gmax_in[pl.ds(lax.rem(mg + k, groups), 1), :])
+    tops[pl.ds(me, 1), :] = jnp.broadcast_to(jnp.max(best, axis=1, keepdims=True), (1, LANES))
+    each_peer(lambda p: outt(p).start())
     slot(recv1, me)[...] = slot(send1, me)[...]
     drain(recv1, r1_sem.at[0], (peers - 2) * 3 * CAP)
     held = collect(me, ((empty,) * 12,) * coarse_groups)
@@ -505,12 +579,6 @@
     for g in range(coarse_groups):
         for n in range(12):
             held_ref[plane_slot(n, g), :] = held[g][n]
-    drain(gmax_in, rg_sem, groups - 1)
-    best = gmax[...]
-    for k in range(1, groups):
-        best = jnp.maximum(best, gmax_in[pl.ds(lax.rem(mg + k, groups), 1), :])
-    tops[pl.ds(me, 1), :] = jnp.broadcast_to(jnp.max(best, axis=1, keepdims=True), (1, LANES))
-    each_peer(lambda p: outt(p).start())
     drain(recv1, r1_sem.at[1], 3 * CAP)
     held = tuple(
         tuple(held_ref[plane_slot(n, g), :] for n in range(12)) for g in range(coarse_groups)
@@ -687,14 +755,8 @@
     )
     step_out[...] = by
 
-    def finish_coarse(i, carry):
-        for g in range(coarse_groups):
-            field, curl, put = blocked(cb, g), blocked(curl_c, g), blocked_put(curl_c, g)
-            for c in range(3):
-                put(c, i, sub2(field(c, i), mul((by, by), curl(c, i))))
-        return carry
-
-    lax.fori_loop(0, EDGE, finish_coarse, 0, unroll=4)
+    for c in range(3):
+        curl_c[c] = cb[c] - by[:1, :1] * curl_c[c]
     twice = 2.0 * by
     tiles = largest_step(fine_count * SPAN // ROWS, 36)
 
@@ -714,7 +776,23 @@
         row = owner_of[r] * ROWS + rank_of[r]
         own_a[r : r + 1, :] = recv2[pl.ds(row, 1), :]
         own_b[r : r + 1, :] = recv2[pl.ds(row + CAP, 1), :]
-    drain(fb, sent_sem, (peers - 1) * (5 * CAP + 1) + groups - 1)
+    drain(fb, sent_sem, (peers - 1) * (2 * CAP + 1) + groups - 1)
+    if relay:
+
+        @pl.when(me == 0)
+        def _():
+            drain(fb, s1_sem, 3 * CAP + (peers - 2) * ROWS)
+
+        @pl.when(me == 1)
+        def _():
+            drain(fb, s1_sem, (2 * peers - 3) * 3 * CAP)
+
+        @pl.when(me > 1)
+        def _():
+            drain(fb, s1_sem, (peers - 1) * 3 * CAP)
+
+    else:
+        drain(fb, s1_sem, (peers - 1) * 3 * CAP)
 
 
 def store(new_c, new_f, fine_face, own_a, own_b, index, step, out_c, out_f, out_j, new_j, sems):
@@ -803,10 +881,14 @@
             vmem((peers * ROWS, LANES), f32),
             vmem((peers * ROWS, LANES), f32),
             vmem((peers * ROWS, LANES), f32),
+            vmem((peers * ROWS, LANES), f32),
             vmem((1, LANES), f32),
             vmem((groups, LANES), f32),
             dma((5,)),
             dma,
+            dma,
+            dma,
+            pltpu.SemaphoreType.REGULAR,
             dma((2,)),
             dma,
             dma,

time: 16.1 us -> 15.8 us (0.981)
  Pallas kernels: 15.3 us -> 15 us
    pallas_call x1, Pallas kernels: 14.2 us -> 13.9 us  [on_device(): pl.pallas_call(functools.partial(kernel, peers, groups, coarse_count, fin...]
where the time goes in v5:
time: 15.8 us; the launch traced here: 15.7 us
  Pallas kernels  15 us (95%)
  between operations  0.64 us (4%)
    pallas_call x1, Pallas kernels, on_device(): pl.pallas_call(functools.partial(kernel, peers, groups, coarse_count, fin...  13.9 us
    pallas_call x1, Pallas kernels, on_device(): pl.pallas_call(store, out_shape=(jax.ShapeDtypeStruct(coarse_shape, f32),...  1.11 us

profile of v5, /device:TPU:0, one launch (start us, length us, event | category | flops | bytes accessed | tf_op | source)
XLA Modules:
  0.0 15.7 jit_solution(17380703080079590711)
XLA Ops:
  0.6 13.9 %shard_map.76 = (f32[3,16,4096]{2,1,0:T(8,128)S(1)}, f32[1152,128]{1,0:T(8,128)S(1)}, f32[16,128]{1,0:T(8,128)S(1)}, f32[8,128]{1,0:T(8,128)S(1)}, f32[8,128]{1,...) custom-call(s32[4,6]{1,0:T(4,128)} %bitcast.18, f32[3,16,4096]{2,1,0:T(8,128)} %bitcast.14, ...), custom_call_target="tpu_custom_call" | custom-call | tf_op jit(solution)/shard_map/pallas_call | solution.py:858
  14.6 1.1 %shard_map.77 = (f32[3,16,4096]{2,1,0:T(8,128)}, f32[1152,128]{1,0:T(8,128)}, f32[4,256]{1,0:T(4,128)}) custom-call(f32[3,16,4096]{2,1,0:T(8,128)S(1)} %get-tuple-element.13.new_c, f32[1152,128]{1,0:T(8,128)S(1)} %get-tuple-element.14.new_f, f32[16,128]{1,0:T(8,128)S(1)} %get-tuple-element.15.fine_face, f32[8,128]{1,0:T(8,128)S(1)} %get-tuple-element.16.own_a, ...), custom_call_target="tpu_custom_call" | custom-call | tf_op jit(solution)/shard_map/pallas_call | solution.py:901

commit v6 on v5

--- a/solution.py
+++ b/solution.py
@@ -354,11 +354,10 @@
         whole = ref.at[pl.ds(0, rows)]
         pltpu.make_async_copy(whole, whole, sem).wait()
 
-    def out_bundle():
-        rows = pl.ds(2 * ROWS, (peers - 2) * ROWS)
+    def hand_over(p):
         return pltpu.make_async_remote_copy(
-            src_ref=send1.at[rows], dst_ref=relayed.at[rows], send_sem=s1_sem,
-            recv_sem=bundle_sem, device_id=(1, mg), device_id_type=MESH,
+            src_ref=part(send1, p, 3 * CAP), dst_ref=part(relayed, p, 3 * CAP), send_sem=s1_sem,
+            recv_sem=bundle_sem.at[min(peers - 1 - p, 2)], device_id=(1, mg), device_id_type=MESH,
         )
 
     def out_relay(p):
@@ -450,23 +449,29 @@
         @pl.when(me == 0)
         def _():
             pl.semaphore_wait(barrier, 1)
+            for p in range(peers - 1, 1, -1):
+                hand_over(p).start()
             out1(1).start()
-            out_bundle().start()
 
         @pl.when(me == 1)
         def _():
             pl.semaphore_wait(barrier, greeted + groups - 1 + peers - 2)
             pl.semaphore_signal(go_sem, inc=1, device_id=(0, mg), device_id_type=MESH)
-            rows = relayed.at[pl.ds(2 * ROWS, (peers - 2) * ROWS)]
-            pltpu.make_async_copy(rows, rows, bundle_sem).wait()
             for p in range(peers - 1, 1, -1):
+                n = peers - 1 - p
+                if n < 2:
+                    drain(relayed, bundle_sem.at[n], 3 * CAP)
+                elif n == 2:
+                    drain(relayed, bundle_sem.at[2], (p - 1) * 3 * CAP)
                 out_relay(p).start()
+                out1(p ^ 1).start()
+            out1(1).start()
 
         @pl.when(jnp.logical_and(me > 1, me < early))
         def _():
             pl.semaphore_wait(barrier, greeted)
 
-        @pl.when(me > 0)
+        @pl.when(me > 1)
         def _():
             send_all()
 
@@ -545,7 +550,12 @@
             fine_put(curl_f, base, fine_curl(fine_edges(fine_read(fb, base), fine_read(fv, base))))
         return carry
 
-    lax.fori_loop(0, fine_count // fine_step, fine_bulk, 0)
+    def fine_all():
+        lax.fori_loop(0, fine_count // fine_step, fine_bulk, 0)
+
+    @pl.when(me < early)
+    def _():
+        fine_all()
 
     def row_of(ref, n):
         return jnp.broadcast_to(ref[pl.ds(n, 1), :], (ROWS, LANES))
@@ -719,6 +729,11 @@
 
     lax.fori_loop(0, EDGE // 4, curl_step, 0)
 
+
+    @pl.when(me >= early)
+    def _():
+        fine_all()
+
     index_n = (lane, k_of, EDGE * k8)
     target_n = (jnp.zeros_like(lane), row16, row16)
 
@@ -779,15 +794,11 @@
     drain(fb, sent_sem, (peers - 1) * (2 * CAP + 1) + groups - 1)
     if relay:
 
-        @pl.when(me == 0)
-        def _():
-            drain(fb, s1_sem, 3 * CAP + (peers - 2) * ROWS)
-
         @pl.when(me == 1)
         def _():
             drain(fb, s1_sem, (2 * peers - 3) * 3 * CAP)
 
-        @pl.when(me > 1)
+        @pl.when(me != 1)
         def _():
             drain(fb, s1_sem, (peers - 1) * 3 * CAP)
 
@@ -887,7 +898,7 @@
             dma((5,)),
             dma,
             dma,
-            dma,
+            dma((3,)),
             pltpu.SemaphoreType.REGULAR,
             dma((2,)),
             dma,

time: 15.8 us -> 15.4 us (0.975)
  Pallas kernels: 15 us -> 14.6 us
    pallas_call x1, Pallas kernels: 13.9 us -> 13.5 us  [on_device(): pl.pallas_call(functools.partial(kernel, peers, groups, coarse_count, fin...]
where the time goes in v6:
time: 15.4 us; the launch traced here: 15.3 us
  Pallas kernels  14.6 us (95%)
  between operations  0.64 us (4%)
    pallas_call x1, Pallas kernels, on_device(): pl.pallas_call(functools.partial(kernel, peers, groups, coarse_count, fin...  13.5 us
    pallas_call x1, Pallas kernels, on_device(): pl.pallas_call(store, out_shape=(jax.ShapeDtypeStruct(coarse_shape, f32),...  1.11 us

profile of v6, /device:TPU:0, one launch (start us, length us, event | category | flops | bytes accessed | tf_op | source)
XLA Modules:
  0.0 15.3 jit_solution(16860284564976665473)
XLA Ops:
  0.6 13.5 %shard_map.76 = (f32[3,16,4096]{2,1,0:T(8,128)S(1)}, f32[1152,128]{1,0:T(8,128)S(1)}, f32[16,128]{1,0:T(8,128)S(1)}, f32[8,128]{1,0:T(8,128)S(1)}, f32[8,128]{1,...) custom-call(s32[4,6]{1,0:T(4,128)} %bitcast.18, f32[3,16,4096]{2,1,0:T(8,128)} %bitcast.14, ...), custom_call_target="tpu_custom_call" | custom-call | tf_op jit(solution)/shard_map/pallas_call | solution.py:869
  14.2 1.1 %shard_map.77 = (f32[3,16,4096]{2,1,0:T(8,128)}, f32[1152,128]{1,0:T(8,128)}, f32[4,256]{1,0:T(4,128)}) custom-call(f32[3,16,4096]{2,1,0:T(8,128)S(1)} %get-tuple-element.13.new_c, f32[1152,128]{1,0:T(8,128)S(1)} %get-tuple-element.14.new_f, f32[16,128]{1,0:T(8,128)S(1)} %get-tuple-element.15.fine_face, f32[8,128]{1,0:T(8,128)S(1)} %get-tuple-element.16.own_a, ...), custom_call_target="tpu_custom_call" | custom-call | tf_op jit(solution)/shard_map/pallas_call | solution.py:912

commit v7 on v6

--- a/solution.py
+++ b/solution.py
@@ -19,7 +19,7 @@
 EMPTY = 3e38
 TANGENT = ((1, 2), (0, 2), (0, 1))
 MESH = pl.DeviceIdType.MESH
-TOP_CHUNK = 4
+TOP_CHUNK = 8
 CHUNK = 4
 CHUNKS = EDGE // CHUNK
 FINE_STEP = 4
@@ -45,7 +45,9 @@
     cv_hbm,
     fb_hbm,
     fv_hbm,
+    cb,
     curl_c,
+    fb,
     curl_f,
     fine_face,
     own_a,
@@ -53,9 +55,7 @@
     index_out,
     step_out,
     pairs,
-    cb,
     cv,
-    fb,
     fv,
     emf_c,
     emf_p,
@@ -75,9 +75,7 @@
     recv2,
     gmax,
     gmax_in,
-    load_sem,
     sent_sem,
-    s1_sem,
     bundle_sem,
     go_sem,
     r1_sem,
@@ -121,6 +119,7 @@
 
     barrier = pltpu.get_barrier_semaphore()
     relay = paired and few and peers > 2
+    near = max(peers - 3, 1)
     early = peers // 2 if relay else 0
     greeted = peers - 1 + groups - 1
 
@@ -129,19 +128,6 @@
         pl.semaphore_signal(barrier, inc=1, device_id=(at, mg), device_id_type=MESH)
 
     each_peer(greet)
-    loads = [
-        pltpu.make_async_copy(src, dst, load_sem.at[n])
-        for n, (src, dst) in enumerate(((fb_hbm, fb), (fv_hbm, fv), (cb_hbm, cb), (cv_hbm, cv)))
-    ]
-    listed = pltpu.make_async_copy(pairs_hbm, pairs, load_sem.at[4])
-    listed.start()
-    for load in loads:
-        load.start()
-    me_or_one = jnp.where(me == 0, 1, me) if relay else me
-    each_group(
-        lambda g: pl.semaphore_signal(barrier, inc=1, device_id=(me_or_one, g), device_id_type=MESH)
-    )
-
     lane = lax.broadcasted_iota(jnp.int32, (ROWS, LANES), 1)
     sub = lax.broadcasted_iota(jnp.int32, (ROWS, LANES), 0)
     zero = jnp.zeros((ROWS, LANES), jnp.float32)
@@ -270,24 +256,8 @@
 
         return put
 
-    loads[0].wait()
-    loads[1].wait()
-
     speed_step = largest_step(fine_count, SPEED_STEP)
-
-    def fine_top(n, best):
-        for u in range(speed_step):
-            base = (n * speed_step + u) * SPAN
-            b, v = fine_read(fb, base), fine_read(fv, base)
-            best = jnp.maximum(best, top_of(v, fine_centre(b)))
-        return best
-
-    best = lax.fori_loop(0, fine_count // speed_step, fine_top, zero)
-
-    loads[2].wait()
-    loads[3].wait()
-
-
+    fine_parts = fine_count // speed_step
     def at(n, i, g, h):
         row = (((n * coarse_groups + g) * EDGE + i) * 2 + h) * ROWS
         return pl.ds(row if isinstance(row, int) else pl.multiple_of(row, ROWS), ROWS)
@@ -297,27 +267,64 @@
             for g in range(coarse_groups):
                 body(chunk * planes + u, g)
 
-    def coarse_top(n, best):
-        tops = []
-
-        def plane(i, g):
-            field = blocked(cb, g)
-            b = [field(c, i) for c in range(3)]
-            c = (
-                add(b[0], field(0, lax.rem(i + 1, EDGE))),
-                add(b[1], ahead_y(b[1])),
-                add(b[2], ahead_z(b[2])),
-            )
-            for k in range(3):
-                for h in range(2):
-                    centred[at(k, i, g, h), :] = c[k][h]
-            tops.append(top_of([blocked(cv, g)(k, i) for k in range(3)], c))
-
-        each_plane(n, TOP_CHUNK, plane)
-        return functools.reduce(jnp.maximum, tops, best)
-
-    best = lax.fori_loop(0, EDGE // TOP_CHUNK, coarse_top, best)
-    gmax[...] = jnp.max(best, axis=0, keepdims=True)
+    def front(load_sem):
+        loads = []
+
+        def load(src, dst):
+            loads.append(pltpu.make_async_copy(src, dst, load_sem.at[1 + len(loads)]))
+
+        for n in range(fine_parts):
+            rows = pl.ds(n * speed_step * SPAN, speed_step * SPAN)
+            load(fb_hbm.at[rows], fb.at[rows])
+            load(fv_hbm.at[rows], fv.at[rows])
+        for g in range(coarse_groups):
+            rows = pl.ds(g * ROWS, ROWS)
+            load(cb_hbm.at[:, rows], cb.at[:, rows])
+            load(cv_hbm.at[:, rows], cv.at[:, rows])
+        listed = pltpu.make_async_copy(pairs_hbm, pairs, load_sem.at[0])
+        listed.start()
+        for copy in loads:
+            copy.start()
+        me_or_one = jnp.where(me == 0, 1, me) if relay else me
+        each_group(
+            lambda g: pl.semaphore_signal(barrier, inc=1, device_id=(me_or_one, g), device_id_type=MESH)
+        )
+
+        best = zero
+        for n in range(fine_parts):
+            loads[2 * n].wait()
+            loads[2 * n + 1].wait()
+            for u in range(speed_step):
+                base = (n * speed_step + u) * SPAN
+                best = jnp.maximum(best, top_of(fine_read(fv, base), fine_centre(fine_read(fb, base))))
+
+
+        def coarse_top(n, best, g):
+            tops = []
+            for u in range(TOP_CHUNK):
+                i = n * TOP_CHUNK + u
+                field = blocked(cb, g)
+                b = [field(c, i) for c in range(3)]
+                c = (
+                    add(b[0], field(0, lax.rem(i + 1, EDGE))),
+                    add(b[1], ahead_y(b[1])),
+                    add(b[2], ahead_z(b[2])),
+                )
+                for k in range(3):
+                    for h in range(2):
+                        centred[at(k, i, g, h), :] = c[k][h]
+                tops.append(top_of([blocked(cv, g)(k, i) for k in range(3)], c))
+            return functools.reduce(jnp.maximum, tops, best)
+
+        for g in range(coarse_groups):
+            loads[2 * fine_parts + 2 * g].wait()
+            loads[2 * fine_parts + 2 * g + 1].wait()
+            best = lax.fori_loop(0, EDGE // TOP_CHUNK, functools.partial(coarse_top, g=g), best)
+        gmax[...] = jnp.max(best, axis=0, keepdims=True)
+        listed.wait()
+
+
+    pl.run_scoped(front, pltpu.SemaphoreType.DMA((1 + 2 * (fine_parts + coarse_groups),)))
 
     def slot(ref, p):
         return ref.at[pl.ds(pl.multiple_of(p * ROWS, ROWS), ROWS)]
@@ -328,8 +335,8 @@
     def out1(k):
         p = target(k)
         return pltpu.make_async_remote_copy(
-            src_ref=part(send1, p, 3 * CAP), dst_ref=part(recv1, me, 3 * CAP), send_sem=s1_sem,
-            recv_sem=r1_sem.at[k // (peers - 1)], device_id=(p, mg), device_id_type=MESH,
+            src_ref=part(send1, p, 3 * CAP), dst_ref=part(recv1, me, 3 * CAP), send_sem=sent_sem,
+            recv_sem=r1_sem.at[k // (near + 1)], device_id=(p, mg), device_id_type=MESH,
         )
 
     def out2(p):
@@ -356,14 +363,14 @@
 
     def hand_over(p):
         return pltpu.make_async_remote_copy(
-            src_ref=part(send1, p, 3 * CAP), dst_ref=part(relayed, p, 3 * CAP), send_sem=s1_sem,
+            src_ref=part(send1, p, 3 * CAP), dst_ref=part(relayed, p, 3 * CAP), send_sem=sent_sem,
             recv_sem=bundle_sem.at[min(peers - 1 - p, 2)], device_id=(1, mg), device_id_type=MESH,
         )
 
     def out_relay(p):
         return pltpu.make_async_remote_copy(
-            src_ref=part(relayed, p, 3 * CAP), dst_ref=part(recv1, 0, 3 * CAP), send_sem=s1_sem,
-            recv_sem=r1_sem.at[p // (peers - 1)], device_id=(p, mg), device_id_type=MESH,
+            src_ref=part(relayed, p, 3 * CAP), dst_ref=part(recv1, 0, 3 * CAP), send_sem=sent_sem,
+            recv_sem=r1_sem.at[p // (near + 1)], device_id=(p, mg), device_id_type=MESH,
         )
 
     def send_all():
@@ -377,8 +384,6 @@
     def _():
         pl.semaphore_wait(barrier, greeted)
         send_group()
-
-    listed.wait()
 
     half_lane = 32 * (row16 % 4)
     index_r = (half_lane + 2 * k8, 2 * k8, half_lane)
@@ -583,17 +588,17 @@
     tops[pl.ds(me, 1), :] = jnp.broadcast_to(jnp.max(best, axis=1, keepdims=True), (1, LANES))
     each_peer(lambda p: outt(p).start())
     slot(recv1, me)[...] = slot(send1, me)[...]
-    drain(recv1, r1_sem.at[0], (peers - 2) * 3 * CAP)
+    drain(recv1, r1_sem.at[0], near * 3 * CAP)
     held = collect(me, ((empty,) * 12,) * coarse_groups)
-    held = each_step(1, peers - 1, lambda k, held: collect(source(k), held), held)
+    held = each_step(1, near + 1, lambda k, held: collect(source(k), held), held)
     for g in range(coarse_groups):
         for n in range(12):
             held_ref[plane_slot(n, g), :] = held[g][n]
-    drain(recv1, r1_sem.at[1], 3 * CAP)
+    drain(recv1, r1_sem.at[1], (peers - 1 - near) * 3 * CAP)
     held = tuple(
         tuple(held_ref[plane_slot(n, g), :] for n in range(12)) for g in range(coarse_groups)
     )
-    held = collect(source(jnp.int32(peers - 1)), held)
+    held = each_step(near + 1, peers, lambda k, held: collect(source(k), held), held)
     spread = row16
     squeeze = EDGE * k8
     upper8 = k_of >= HALF
@@ -770,18 +775,8 @@
     )
     step_out[...] = by
 
-    for c in range(3):
-        curl_c[c] = cb[c] - by[:1, :1] * curl_c[c]
+    curl_c[0] = cb[0] - by[:1, :1] * curl_c[0]
     twice = 2.0 * by
-    tiles = largest_step(fine_count * SPAN // ROWS, 36)
-
-    def finish_fine(n, carry):
-        for u in range(tiles):
-            rows = pl.ds(pl.multiple_of((n * tiles + u) * ROWS, ROWS), ROWS)
-            curl_f[rows, :] = fb[rows, :] - twice * curl_f[rows, :]
-        return carry
-
-    lax.fori_loop(0, fine_count * SPAN // ROWS // tiles, finish_fine, 0)
     for n in range(0, 2 * pair_rows, ROWS):
         far = slice(2 * pair_rows + n, 2 * pair_rows + n + ROWS)
         fine_face[n : n + ROWS, :] = picked[n : n + ROWS, :] - twice * picked[far, :]
@@ -791,28 +786,37 @@
         row = owner_of[r] * ROWS + rank_of[r]
         own_a[r : r + 1, :] = recv2[pl.ds(row, 1), :]
         own_b[r : r + 1, :] = recv2[pl.ds(row + CAP, 1), :]
-    drain(fb, sent_sem, (peers - 1) * (2 * CAP + 1) + groups - 1)
+    other = (peers - 1) * (2 * CAP + 1) + groups - 1
     if relay:
 
         @pl.when(me == 1)
         def _():
-            drain(fb, s1_sem, (2 * peers - 3) * 3 * CAP)
+            drain(fb, sent_sem, other + (2 * peers - 3) * 3 * CAP)
 
         @pl.when(me != 1)
         def _():
-            drain(fb, s1_sem, (peers - 1) * 3 * CAP)
+            drain(fb, sent_sem, other + (peers - 1) * 3 * CAP)
 
     else:
-        drain(fb, s1_sem, (peers - 1) * 3 * CAP)
-
-
-def store(new_c, new_f, fine_face, own_a, own_b, index, step, out_c, out_f, out_j, new_j, sems):
-    copies = [
-        pltpu.make_async_copy(src, dst, sems.at[n])
-        for n, (src, dst) in enumerate(((new_c, out_c), (new_f, out_f)))
-    ]
-    for copy in copies:
-        copy.start()
+        drain(fb, sent_sem, other + (peers - 1) * 3 * CAP)
+
+
+def store(
+    cb, curl_c, fb, curl_f, fine_face, own_a, own_b, index, step, out_c, out_f, out_j, new_c, new_f, new_j, sems
+):
+    by = step[0:1, 0:1]
+    copies = []
+
+    def send(src, dst):
+        copies.append(pltpu.make_async_copy(src, dst, sems.at[len(copies)]))
+        copies[-1].start()
+
+    send(curl_c.at[0], out_c.at[0])
+    for c in range(1, 3):
+        new_c[c - 1] = cb[c] - by * curl_c[c]
+        send(new_c.at[c - 1], out_c.at[c])
+    new_f[...] = fb[...] - (2.0 * by) * curl_f[...]
+    send(new_f, out_f)
     count, pair_rows = out_j.shape[0], own_a.shape[0]
     for s in range(0, count, ROWS):
         coarse = own_b[s : s + ROWS, :] - step[...] * own_a[s : s + ROWS, :]
@@ -821,8 +825,7 @@
             new_j[s : s + ROWS, h * LANES : (h + 1) * LANES] = fine_face[here, :] - take(
                 coarse, index[here, :]
             )
-    copies.append(pltpu.make_async_copy(new_j.at[pl.ds(0, count)], out_j, sems.at[2]))
-    copies[-1].start()
+    send(new_j.at[pl.ds(0, count)], out_j)
     for copy in copies:
         copy.wait()
 
@@ -858,6 +861,8 @@
     coarse_shape, fine_shape = (3, coarse_count, cells), (flat_rows, LANES)
     shapes = (
         coarse_shape,
+        coarse_shape,
+        fine_shape,
         fine_shape,
         (2 * pair_rows, LANES),
         (pair_rows, LANES),
@@ -865,7 +870,7 @@
         (2 * pair_rows, LANES),
         (ROWS, LANES),
     )
-    kinds = [f32] * 5 + [jnp.int32, f32]
+    kinds = [f32] * 7 + [jnp.int32, f32]
     results = pl.pallas_call(
         functools.partial(kernel, peers, groups, coarse_count, fine_count, pair_count),
         out_shape=tuple(jax.ShapeDtypeStruct(s, k) for s, k in zip(shapes, kinds)),
@@ -874,8 +879,6 @@
         scratch_shapes=[
             pltpu.SMEM(pairs.shape[1:], jnp.int32),
             vmem(coarse_shape, f32),
-            vmem(coarse_shape, f32),
-            vmem(fine_shape, f32),
             vmem(fine_shape, f32),
             vmem(coarse_shape, f32),
             vmem((pair_count * SPAN, LANES), f32),
@@ -895,8 +898,6 @@
             vmem((peers * ROWS, LANES), f32),
             vmem((1, LANES), f32),
             vmem((groups, LANES), f32),
-            dma((5,)),
-            dma,
             dma,
             dma((3,)),
             pltpu.SemaphoreType.REGULAR,
@@ -919,8 +920,10 @@
         in_specs=[inside] * len(shapes),
         out_specs=(anywhere,) * 3,
         scratch_shapes=[
+            vmem((2, coarse_count, cells), f32),
+            vmem(fine_shape, f32),
             vmem((pair_rows, EDGE * EDGE), f32),
-            dma((3,)),
+            dma((5,)),
         ],
     )(*(pltpu.with_memory_space_constraint(x, pltpu.VMEM) for x in results))
     return (

time: 15.4 us -> 15.4 us (level)
  no operation moved by 1% of the time
where the time goes in v7:
time: 15.4 us; the launch traced here: 15.2 us
  Pallas kernels  14.6 us (95%)
  between operations  0.64 us (4%)
    pallas_call x1, Pallas kernels, on_device(): pl.pallas_call(functools.partial(kernel, peers, groups, coarse_count, fin...  13.4 us
    pallas_call x1, Pallas kernels, on_device(): pl.pallas_call(store, out_shape=(jax.ShapeDtypeStruct(coarse_shape, f32),...  1.13 us

profile of v7, /device:TPU:0, one launch (start us, length us, event | category | flops | bytes accessed | tf_op | source)
XLA Modules:
  0.0 15.2 jit_solution(7310001179671002546)
XLA Ops:
  0.6 13.4 %shard_map.76 = (f32[3,16,4096]{2,1,0:T(8,128)S(1)}, f32[3,16,4096]{2,1,0:T(8,128)S(1)}, f32[1152,128]{1,0:T(8,128)S(1)}, f32[1152,128]{1,0:T(8,128)S(1)}, f32[1...) custom-call(s32[4,6]{1,0:T(4,128)} %bitcast.18, ...), custom_call_target="tpu_custom_call" | custom-call | tf_op jit(solution)/shard_map/pallas_call | solution.py:874
  14.1 1.1 %shard_map.77 = (f32[3,16,4096]{2,1,0:T(8,128)}, f32[1152,128]{1,0:T(8,128)}, f32[4,256]{1,0:T(4,128)}) custom-call(f32[3,16,4096]{2,1,0:T(8,128)S(1)} %get-tuple-element.15.cb, f32[3,16,4096]{2,1,0:T(8,128)S(1)} %get-tuple-element.16.curl_c, f32[1152,128]{1,0:T(8,128)S(1)} %get-tuple-element.17.fb, f32[1152,128]{1,0:T(8,128)S(1)} %get-tuple-element.18.curl_f, ...), custom_call_target="tpu_custom_call" | custom-call | tf_op jit(solution)/shard_map/pallas_call | solution.py:913
